TPU v7x, 512 devices: a whole 4x8x8 slice. The times are simulated.
512 devices in a mesh: pipe: 16 (over z, core), ctx: 32 (over y, x).
Axes of the slice: x: 4, y: 8, z: 8, core: 2. Of those that a mesh axis runs over, the one named last changes fastest.
Arguments:
- states: bfloat16 [16, 4096, 2048], P('pipe', 'ctx'), may hold values from -6 to 6
- norm_gain: float32 [16, 2048], P('pipe'), may hold values from 0.25 to 1.75
- w_in: bfloat16 [16, 2048, 1536], P('pipe', 'ctx'), may hold values from -1 to 1
- w_out: bfloat16 [16, 1024, 2048], P('pipe', 'ctx'), may hold values from -0.1875 to 0.1875
- lengths: int32 [16, 8], replicated, may hold values from 1 to 1024, 4096 in all within a row
Outputs:
- moved: bfloat16 [16, 4096, 2048], P('pipe', 'ctx')
Inputs may be any that keep to these rules, and one draw needn't show every extreme that they name: Each row of lengths lays the responses of one micro-batch end to end over the 4096 positions.
All inputs are finite; a program needn't handle non-finite values.
Results may differ from a plain program's by a relative error of at most 0.0045.
Values may be sent and summed in bfloat16 or wider, within the bound.
A program may use at most 64 MiB of HBM per device.

v0:
```python
import jax
import jax.numpy as jnp
from jax import lax
from jax.sharding import Mesh
from jax.sharding import PartitionSpec as P

HEAD_DIM = 64
HEADS = 16
KV_HEADS = 4
CTX = ("ctx_0", "ctx_1")


epsilon = 1e-05
rope_base = 500000.0
masked_score = -1e30


def whole_of(x, axes, dim):
    result = x
    for number in range(len(axes) - 1, -1, -1):
        result = lax.all_gather(result, axes[number], axis=dim, tiled=True)
    return result


def passed_along(value, axis, steps):
    count = lax.axis_size(axis)
    initial, last = (max(0, -steps), min(count, count - steps))
    return lax.ppermute(value, axis, [(source, source + steps) for source in range(initial, last)])


def passed_along_2(value, axis, steps):
    count = lax.axis_size(axis)
    pairs = [(source, (source + steps) % count) for source in range(count)]
    return lax.ppermute(value, axis, pairs)


def locate(doc_lengths, spots):
    doc_ends = jnp.cumsum(doc_lengths)
    segment = jnp.sum((doc_ends[None, :] <= spots[:, None]).astype(jnp.int32), axis=1)
    starts = doc_ends - doc_lengths
    labels = jnp.arange(doc_lengths.shape[0], dtype=jnp.int32)
    first = jnp.sum(jnp.where(segment[:, None] == labels[None, :], starts[None, :], 0), axis=1)
    return (segment, spots - first)


def rotate_pairs(heads_data, position):
    half_dim = heads_data.shape[-1] // 2
    inverse = rope_base ** (-jnp.arange(half_dim, dtype=jnp.float32) * 2.0 / heads_data.shape[-1])
    angles = position.astype(jnp.float32)[:, None] * inverse[None, :]
    cosine = jnp.cos(angles)[:, None, :]
    sine_part = jnp.sin(angles)[:, None, :]
    first_half = heads_data[..., :half_dim]
    second_half = heads_data[..., half_dim:]
    return jnp.concatenate(
        [
            first_half * cosine - second_half * sine_part,
            second_half * cosine + first_half * sine_part,
        ],
        -1,
    )


def body(states, norm_gain, w_in, w_out, lengths):
    section_index = lax.axis_index("pipe")
    ctx_index = lax.axis_index(CTX)
    ctx_count = lax.axis_size(CTX)
    tok_rows = states.shape[1]
    doc_lengths = lax.dynamic_index_in_dim(lengths, section_index, 0, keepdims=False)
    gain = norm_gain[0]
    weight_in = w_in[0]
    weight_out = w_out[0]
    wide = states[0].astype(jnp.float32)
    normed = (wide * lax.rsqrt(jnp.mean(wide * wide, -1, keepdims=True) + epsilon) * gain).astype(
        jnp.bfloat16
    )
    columns = normed
    proj = jnp.dot(columns, whole_of(weight_in, CTX, 0), preferred_element_type=jnp.float32)
    q_width = HEADS * HEAD_DIM
    k_width = KV_HEADS * HEAD_DIM
    group = HEADS // KV_HEADS
    first_spot = ctx_index * tok_rows
    query_spots = first_spot + jnp.arange(tok_rows, dtype=jnp.int32)
    query_seg, position = locate(doc_lengths, query_spots)
    queries = rotate_pairs(proj[:, :q_width].reshape(tok_rows, HEADS, HEAD_DIM), position).astype(
        jnp.bfloat16
    )
    queries = queries.reshape(tok_rows, KV_HEADS, group, HEAD_DIM)
    keys_rot = rotate_pairs(
        proj[:, q_width : q_width + k_width].reshape(tok_rows, KV_HEADS, HEAD_DIM), position
    ).astype(jnp.bfloat16)
    values = proj[:, q_width + k_width :].astype(jnp.bfloat16)
    key_values = jnp.concatenate([keys_rot.reshape(tok_rows, k_width), values], 1)

    def attend_block(carry, portion, offset):
        row_count = portion.shape[0]
        key_spots = offset + jnp.arange(row_count, dtype=jnp.int32)
        key_seg, unused_place = locate(doc_lengths, key_spots)
        allowed = (
            (query_seg[:, None] == key_seg[None, :])
            & (key_spots[None, :] <= query_spots[:, None])
            & (key_spots[None, :] >= 0)
        )

        def update(state):
            running_max, running_sum, accum = state
            key_part = portion[:, :k_width].reshape(row_count, KV_HEADS, HEAD_DIM)
            value_part = portion[:, k_width:].reshape(row_count, KV_HEADS, HEAD_DIM)
            scores = jnp.einsum(
                "tgjd,rgd->gjtr", queries, key_part, preferred_element_type=jnp.float32
            ) * HEAD_DIM ** (-0.5)
            scores = jnp.where(allowed, scores, masked_score)
            new_max = jnp.maximum(running_max, jnp.max(scores, -1))
            rescale = jnp.exp(running_max - new_max)
            probs = jnp.where(allowed, jnp.exp(scores - new_max[..., None]), 0.0)
            new_sum = running_sum * rescale + jnp.sum(probs, -1)
            product = jnp.einsum(
                "gjtr,rgd->gjtd",
                probs.astype(jnp.bfloat16),
                value_part,
                preferred_element_type=jnp.float32,
            )
            return (new_max, new_sum, accum * rescale[..., None] + product)

        return lax.cond(jnp.any(allowed), update, lambda state: state, carry)

    initial = (
        jnp.full((KV_HEADS, group, tok_rows), masked_score, jnp.float32),
        jnp.zeros((KV_HEADS, group, tok_rows), jnp.float32),
        jnp.zeros((KV_HEADS, group, tok_rows, HEAD_DIM), jnp.float32),
    )
    resp_longest = min(1024, 8 * tok_rows, tok_rows * ctx_count // 2)
    reach_count = min(ctx_count - 1, (resp_longest + tok_rows - 2) // tok_rows)
    needed = reach_count + 1
    collected = key_values
    held = 1
    while held < needed:
        taken = min(held, needed - held)
        arrived = passed_along(collected[collected.shape[0] - taken * tok_rows :], CTX, held)
        collected = jnp.concatenate([arrived, collected], 0)
        held = held + taken
    carry = initial
    portion = collected
    offset = first_spot - (held - 1) * tok_rows
    row_count = portion.shape[0]
    block_rows = min(row_count, 512)
    full_blocks = row_count // block_rows

    def visit_block(block_idx, state):
        sliced = lax.dynamic_slice_in_dim(portion, block_idx * block_rows, block_rows, 0)
        return attend_block(state, sliced, offset + block_idx * block_rows)

    carry = lax.fori_loop(0, full_blocks, visit_block, carry)
    carry = attend_block(
        carry, portion[full_blocks * block_rows :], offset + full_blocks * block_rows
    )
    running_max, running_sum, accum = carry
    attended = (
        (accum / running_sum[..., None])
        .transpose(2, 0, 1, 3)
        .reshape(tok_rows, q_width)
        .astype(jnp.bfloat16)
    )
    columns = attended
    output = jnp.dot(columns, whole_of(weight_out, CTX, 0), preferred_element_type=jnp.float32)
    new_state = (wide + output).astype(jnp.bfloat16)
    passed = passed_along_2(new_state, "pipe", 1)
    return passed[None]


def solution(mesh):
    finer = Mesh(mesh.devices.reshape(mesh.shape["pipe"], 8, 4), ("pipe", "ctx_0", "ctx_1"))
    placed = (
        P("pipe", CTX, None),
        P("pipe", None),
        P("pipe", CTX, None),
        P("pipe", CTX, None),
        P(),
    )
    return jax.shard_map(
        body, mesh=finer, in_specs=placed, out_specs=P("pipe", CTX, None), check_vma=False
    )
```

profile of v0, /device:TPU:40, one launch (start us, length us, event | category | flops | bytes accessed | tf_op | source)
XLA Modules:
  0.0 208.0 jit_solution(7072770781254716281)
XLA Ops:
  6.5 16.1 %all-gather = bf16[1,256,1536]{2,1,0:T(8,128)(2,1)} all-gather(bf16[1,64,1536]{2,1,0:T(8,128)(2,1)} %param.13), channel_id=2, replica_groups=mesh['pipe'=16,'ctx_0'=8,'ctx_1'=4] {'ctx_1'}, dimensions={1}, use_global_device_ids=true | all-gather | bytes 983040 | tf_op jit(solution)/shard_map/all_gather | solution.py:21
  22.7 13.7 %all-gather.2 = bf16[1,128,2048]{2,1,0:T(8,128)(2,1)} all-gather(bf16[1,32,2048]{2,1,0:T(8,128)(2,1)} %param.14), channel_id=4, replica_groups=mesh['pipe'=16,'ctx_0'=8,'ctx_1'=4] {'ctx_1'}, dimensions={1}, use_global_device_ids=true | all-gather | bytes 655360 | tf_op jit(solution)/shard_map/all_gather | solution.py:21
  37.1 1.2 fusion.34
  38.4 62.4 %all-gather.7.cloned.1.call-done = bf16[1,2048,1536]{2,1,0:T(8,128)(2,1)} async-done(((bf16[1,256,1536]{2,1,0:T(8,128)(2,1)}), bf16[1,2048,1536]{2,1,0:T(8,128)(2,1)}) %all-gather.7.cloned.1.call-update) | async-done | bytes 6291472 | tf_op jit(solution)/shard_map/all_gather | solution.py:21
  100.8 4.0 %fusion.24 = f32[128,1536]{1,0:T(8,128)S(1)} fusion(bf16[1,2048,1536]{2,1,0:T(8,128)(2,1)} %all-gather.7.cloned.1.call-done, bf16[1,128,2048]{2,1,0:T(8,128)(2,1)} %param.11, f32[2048]{0:T(1024)} %bitcast.119, f32[128]{0:T(128)S(1)} %add_rsqrt_fusion), kind=kOutput, calls=%fused_computation.34 | convolution fusion | flops 806354944 | bytes 7610880 | tf_op jit(solution)/shard_map/dot_general | solution.py:77
  105.2 3.4 %collective-permute-start.1 = (bf16[128,512]{1,0:T(8,128)(2,1)S(1)}, bf16[128,512]{1,0:T(8,128)(2,1)S(1)}, u32[]{:S(2)}, u32[]{:S(2)}) collective-permute-start(bf16[128,512]{1,0:T(8,128)(2,1)S(1)} %pad_maximum_fusion.1), channel_id=1, source_target_pairs={{0,1},{1,2},{2,3},{3,4},{4,5},{5,6},{6,7},{7,8},{8,9},{9,10},{10,1... | collective-permute-start | bytes 393224 | tf_op jit(solution)/shard_map/ppermute | solution.py:28
  108.5 5.7 %collective-permute-done.1 = bf16[128,512]{1,0:T(8,128)(2,1)S(1)} collective-permute-done((bf16[128,512]{1,0:T(8,128)(2,1)S(1)}, bf16[128,512]{1,0:T(8,128)(2,1)S(1)}, u32[]{:S(2)}, u32[]{:S(2)}) %collective-permute-start.1) | collective-permute-done | bytes 131104 | tf_op jit(solution)/shard_map/ppermute | solution.py:28
  114.2 2.8 %collective-permute-start.2 = (bf16[256,512]{1,0:T(8,128)(2,1)S(1)}, bf16[256,512]{1,0:T(8,128)(2,1)S(1)}, u32[]{:S(2)}, u32[]{:S(2)}) collective-permute-start(bf16[256,512]{1,0:T(8,128)(2,1)S(1)} %maximum_maximum_fusion.1), channel_id=1, source_target_pairs={{0,2},{1,3},{2,4},{3,5},{4,6},{5,7},{6,8},{7,9},{8,10},{9,11},{10,... | collective-permute-start | bytes 786440 | tf_op jit(solution)/shard_map/ppermute | solution.py:28
  117.0 15.1 %collective-permute-done.2 = bf16[256,512]{1,0:T(8,128)(2,1)S(1)} collective-permute-done((bf16[256,512]{1,0:T(8,128)(2,1)S(1)}, bf16[256,512]{1,0:T(8,128)(2,1)S(1)}, u32[]{:S(2)}, u32[]{:S(2)}) %collective-permute-start.2) | collective-permute-done | bytes 262176 | tf_op jit(solution)/shard_map/ppermute | solution.py:28
  132.2 2.5 %collective-permute-start.3 = (bf16[512,512]{1,0:T(8,128)(2,1)S(1)}, bf16[512,512]{1,0:T(8,128)(2,1)S(1)}, u32[]{:S(2)}, u32[]{:S(2)}) collective-permute-start(bf16[512,512]{1,0:T(8,128)(2,1)S(1)} %maximum_maximum_fusion), channel_id=1, source_target_pairs={{0,4},{1,5},{2,6},{3,7},{4,8},{5,9},{6,10},{7,11},{8,12},{9,13},{1... | collective-permute-start | bytes 1572872 | tf_op jit(solution)/shard_map/ppermute | solution.py:28
  134.6 0.8 and_and_fusion.1
  136.3 1.9 collective-permute-start
  138.6 33.0 %collective-permute-done = bf16[128,512]{1,0:T(8,128)(2,1)S(1)} collective-permute-done((bf16[128,512]{1,0:T(8,128)(2,1)S(1)}, bf16[128,512]{1,0:T(8,128)(2,1)S(1)}, u32[]{:S(2)}, u32[]{:S(2)}) %collective-permute-start) | collective-permute-done | bytes 131104 | tf_op jit(solution)/shard_map/ppermute | solution.py:28
  172.2 0.8 constant_dynamic-update-slice_fusion.3
  173.0 0.7 constant_dynamic-update-slice_fusion.2
  173.7 0.7 constant_dynamic-update-slice_fusion.1
  175.1 1.7 copy.32
  176.8 9.5 %while.20 = (s32[]{:T(128)}, f32[4,4,128]{2,1,0:T(4,128)S(1)}, f32[4,4,128]{2,1,0:T(4,128)S(1)}, f32[4,4,128,64]{2,3,1,0:T(8,128)S(1)}, s32[128]{0:T(128)S(1)}, ...) while((s32[]{:T(128)}, f32[4,4,128]{2,1,0:T(4,128)S(1)}, ...), condition=%wide.region_13.14_spmd.clone, body=%wide.region_6.13_spmd.clone.sunk | while | flops 282674304 | bytes 15872869 | solution.py:152
  177.0 0.9 fusion.53
  178.5 3.1 %conditional.5 = ((f32[4,4,128]{2,1,0:T(4,128)S(1)}, f32[4,4,128]{2,1,0:T(4,128)S(1)}, f32[4,4,128,64]{2,3,1,0:T(8,128)S(1)})) conditional(s32[]{:T(128)} %convert_element_type.103, (f32[4,4,128]{2,1,0:T(4,128)S(1)}, f32[4,4,128]{2,1,0:T(4,128)S(1)}, f32[4,4,128,64]{2,3,1,0:T(8,128)S(1)}) %tuple.82, (pred[128,512]{0,1:T(8,128)(4,1)S(1)}, s32[]{:T(128)}, ...), branch_computations={%region_9.9_spmd, %region_10.12_spmd} | conditional | flops 282333184 | bytes 15794262 | solution.py:124
  178.6 0.8 fusion.2
  179.4 1.0 fusion.4
  180.4 1.2 fusion.8
  181.7 0.9 fusion.53
  183.3 3.1 %conditional.5 = ((f32[4,4,128]{2,1,0:T(4,128)S(1)}, f32[4,4,128]{2,1,0:T(4,128)S(1)}, f32[4,4,128,64]{2,3,1,0:T(8,128)S(1)})) conditional(s32[]{:T(128)} %convert_element_type.103, (f32[4,4,128]{2,1,0:T(4,128)S(1)}, f32[4,4,128]{2,1,0:T(4,128)S(1)}, f32[4,4,128,64]{2,3,1,0:T(8,128)S(1)}) %tuple.82, (pred[128,512]{0,1:T(8,128)(4,1)S(1)}, s32[]{:T(128)}, ...), branch_computations={%region_9.9_spmd, %region_10.12_spmd} | conditional | flops 282333184 | bytes 15794262 | solution.py:124
  183.4 0.8 fusion.2
  184.1 1.0 fusion.4
  185.2 1.2 fusion.8
  186.4 1.1 conditional.2
  187.6 2.9 %fusion.31 = bf16[128,2048]{1,0:T(8,128)(2,1)S(1)} fusion(bf16[128,1024]{0,1:T(8,128)(2,1)S(1)} %bitcast.102, bf16[1,1024,2048]{2,1,0:T(8,128)(2,1)} %all-gather.9.cloned.1.call-done, bf16[1,128,2048]{2,1,0:T(8,128)(2,1)S(1)} %copy-done.1), kind=kOutput, calls=%fused_computation.39 | convolution fusion | flops 537657344 | bytes 5505024 | tf_op jit(solution)/shard_map/dot_general | solution.py:164
  190.6 9.8 %collective-permute-done.4 = bf16[128,2048]{1,0:T(8,128)(2,1)S(1)} collective-permute-done((bf16[128,2048]{1,0:T(8,128)(2,1)S(1)}, bf16[128,2048]{1,0:T(8,128)(2,1)S(1)}, u32[]{:S(2)}, u32[]{:S(2)}) %collective-permute-start.4) | collective-permute-done | bytes 524320 | tf_op jit(solution)/shard_map/ppermute | solution.py:34
  200.4 0.8 copy.70
  (65 shorter events, 4.4 us)
Async XLA Ops:
  6.5 30.0 %copy-start = (s32[16,8]{0,1:T(8,128)S(1)}, s32[16,8]{0,1:T(8,128)}, u32[]{:S(2)}) copy-start(s32[16,8]{0,1:T(8,128)} %param.15) | copy-start | bytes 1540
  6.5 94.3 %all-gather.7.cloned.1.call-start = ((), (), s32[]{:S(2)}) async-start(), calls=%async_computation | async-start | bytes 7077888 | tf_op jit(solution)/shard_map/all_gather | solution.py:21
  22.7 164.9 %all-gather.9.cloned.1.call-start = ((), (), s32[]{:S(2)}) async-start(), calls=%async_computation.1 | async-start | bytes 4718592 | tf_op jit(solution)/shard_map/all_gather | solution.py:21
  105.2 9.1 %collective-permute-start.1 = (bf16[128,512]{1,0:T(8,128)(2,1)S(1)}, bf16[128,512]{1,0:T(8,128)(2,1)S(1)}, u32[]{:S(2)}, u32[]{:S(2)}) collective-permute-start(bf16[128,512]{1,0:T(8,128)(2,1)S(1)} %pad_maximum_fusion.1), channel_id=1, source_target_pairs={{0,1},{1,2},{2,3},{3,4},{4,5},{5,6},{6,7},{7,8},{8,9},{9,10},{10,1... | collective-permute-start | bytes 393224 | tf_op jit(solution)/shard_map/ppermute | solution.py:28
  114.2 17.9 %collective-permute-start.2 = (bf16[256,512]{1,0:T(8,128)(2,1)S(1)}, bf16[256,512]{1,0:T(8,128)(2,1)S(1)}, u32[]{:S(2)}, u32[]{:S(2)}) collective-permute-start(bf16[256,512]{1,0:T(8,128)(2,1)S(1)} %maximum_maximum_fusion.1), channel_id=1, source_target_pairs={{0,2},{1,3},{2,4},{3,5},{4,6},{5,7},{6,8},{7,9},{8,10},{9,11},{10,... | collective-permute-start | bytes 786440 | tf_op jit(solution)/shard_map/ppermute | solution.py:28
  132.2 40.0 %collective-permute-start.3 = (bf16[512,512]{1,0:T(8,128)(2,1)S(1)}, bf16[512,512]{1,0:T(8,128)(2,1)S(1)}, u32[]{:S(2)}, u32[]{:S(2)}) collective-permute-start(bf16[512,512]{1,0:T(8,128)(2,1)S(1)} %maximum_maximum_fusion), channel_id=1, source_target_pairs={{0,4},{1,5},{2,6},{3,7},{4,8},{5,9},{6,10},{7,11},{8,12},{9,13},{1... | collective-permute-start | bytes 1572872 | tf_op jit(solution)/shard_map/ppermute | solution.py:28
  136.3 35.2 %collective-permute-start = (bf16[128,512]{1,0:T(8,128)(2,1)S(1)}, bf16[128,512]{1,0:T(8,128)(2,1)S(1)}, u32[]{:S(2)}, u32[]{:S(2)}) collective-permute-start(bf16[128,512]{1,0:T(8,128)(2,1)S(1)} %pad_maximum_fusion.1), channel_id=1, source_target_pairs={{0,8},{1,9},{2,10},{3,11},{4,12},{5,13},{6,14},{7,15},{8,16},{9,17... | collective-permute-start | bytes 393224 | tf_op jit(solution)/shard_map/ppermute | solution.py:28
  186.4 1.2 copy-start.1
  190.5 9.8 %collective-permute-start.4 = (bf16[128,2048]{1,0:T(8,128)(2,1)S(1)}, bf16[128,2048]{1,0:T(8,128)(2,1)S(1)}, u32[]{:S(2)}, u32[]{:S(2)}) collective-permute-start(bf16[128,2048]{1,0:T(8,128)(2,1)S(1)} %fusion.31), channel_id=1, source_target_pairs={{0,32},{32,64},{64,96},{96,128},{128,160},{160,192},{192,224},{224... | collective-permute-start | bytes 1572872 | tf_op jit(solution)/shard_map/ppermute | solution.py:34
Sparse Core Ops, SparseCore 0:
  22.8 77.9 all-gather.6
  102.9 72.9 all-gather.8
where the time goes:
time: 208 us
  waiting for transfers between devices  126 us (61%)
  blocking collectives  29.9 us (14%)
  between operations  14.3 us (7%)
  matrix products  11.6 us (6%)
  starting transfers between devices  10.6 us (5%)
  other arithmetic  7.95 us (4%)
  local copies, waits for them, and re-layouts  6.18 us (3%)
    all_gather x2, waiting for transfers between devices, whole_of(): result = lax.all_gather(result, axes[number], axis=dim, tiled=True)  62.4 us
    ppermute x4, waiting for transfers between devices, passed_along(): lax.ppermute(value, axis, [(source, source + steps) for source in range(i...  53.7 us
    all_gather x2, blocking collectives, whole_of(): result = lax.all_gather(result, axes[number], axis=dim, tiled=True)  29.9 us
    ppermute x4, starting transfers between devices, passed_along(): lax.ppermute(value, axis, [(source, source + steps) for source in range(i...  10.5 us
    ppermute x1, waiting for transfers between devices, passed_along_2(): return lax.ppermute(value, axis, pairs)  9.8 us
    unnamed x11, local copies, waits for them, and re-layouts  5.41 us
  transfers between devices with their start and end apart: 7, of which 5 were waited for; matrix products, arithmetic and copies ran while one was open for 11% of the time, Pallas kernels for 0%

commit v1 on v0

v1 whole, which is shorter than its diff:
```python
import functools
import math

import jax
import jax.numpy as jnp
from jax import lax
from jax.experimental import pallas as pl
from jax.experimental.pallas import tpu as pltpu
from jax.sharding import Mesh
from jax.sharding import PartitionSpec as P

HEAD_DIM = 64
HEADS = 16
KV_HEADS = 4
GROUP = HEADS // KV_HEADS
NX = 4
CHUNKS = 2
WINDOW = 9
COLS = (GROUP + 2) * HEAD_DIM

epsilon = 1e-05
rope_base = 500000.0
masked_score = -1e30
MESH = pl.DeviceIdType.MESH


def sine_cosine(angle):
    turns = jnp.floor(angle * (2.0 / math.pi) + 0.5)
    quarter = turns.astype(jnp.int32)
    rest = angle - turns * 1.5703125
    rest = rest - turns * 4.837512969970703125e-4
    rest = rest - turns * 7.54978995489188216e-8
    z = rest * rest
    sine = ((-1.9515295891e-4 * z + 8.3321608736e-3) * z - 1.6666654611e-1) * z * rest + rest
    cosine = (
        (2.443315711809948e-5 * z - 1.388731625493765e-3) * z + 4.166664568298827e-2
    ) * z * z - 0.5 * z + 1.0
    odd = (quarter & 1) == 1
    sine, cosine = jnp.where(odd, cosine, sine), jnp.where(odd, sine, cosine)
    sine = jnp.where((quarter & 2) == 2, -sine, sine)
    cosine = jnp.where(((quarter + 1) & 2) == 2, -cosine, cosine)
    return sine, cosine


def response_start(ends, spots):
    start = jnp.zeros_like(spots)
    for end in ends:
        start = jnp.maximum(start, jnp.where(spots >= end, end, 0))
    return start


def tick_kernel(
    n_pipe,
    n_y,
    lengths,
    inverse,
    gain,
    x_hbm,
    wi_hbm,
    wo_hbm,
    out,
    xg,
    xn,
    wloc,
    wsp,
    wi,
    wo,
    trig,
    q_s,
    kv,
    att,
    acc,
    obuf,
    local_sem,
    send_sem,
    recv_sem,
):
    p = lax.axis_index("pipe")
    y = lax.axis_index("ctx_y")
    x = lax.axis_index("ctx_x")
    rows = xg.shape[1]
    half = rows // 2
    part = rows // CHUNKS
    depth = xg.shape[2]
    out_cols = acc.shape[1]
    span = NX * rows

    def xs(d):
        return lax.rem(x + (d + NX), NX)

    def ys(d):
        return lax.rem(y + (d + n_y), n_y)

    def ps(d):
        return lax.rem(p + (d + n_pipe), n_pipe)

    counter = [0]
    pending = []

    def send(src, dst, device, landing=None):
        k = counter[0]
        counter[0] += 1
        copy = pltpu.make_async_remote_copy(
            src_ref=src,
            dst_ref=dst,
            send_sem=send_sem.at[k],
            recv_sem=recv_sem.at[k],
            device_id=device,
            device_id_type=MESH,
        )
        copy.start()
        pending.append(copy)
        land = dst if landing is None else landing

        def arrive():
            pltpu.make_async_remote_copy(
                src_ref=land,
                dst_ref=land,
                send_sem=send_sem.at[k],
                recv_sem=recv_sem.at[k],
                device_id=device,
                device_id_type=MESH,
            ).wait_recv()

        return arrive

    load_w = pltpu.make_async_copy(wi_hbm, wloc, local_sem.at[0])
    load_x = pltpu.make_async_copy(x_hbm, xg.at[0], local_sem.at[1])
    own_cols = pl.ds(pl.multiple_of(x * out_cols, out_cols), out_cols)
    load_o = pltpu.make_async_copy(
        wo_hbm.at[:, own_cols], wo.at[y, x // 2, lax.rem(x, 2)], local_sem.at[2]
    )
    load_w.start()
    load_x.start()
    load_o.start()

    barrier = pltpu.get_barrier_semaphore()
    peers = [(p, y, xs(d)) for d in (1, 2, 3)]
    peers += [(p, ys(d), x) for d in (1, -1)]
    peers += [(ps(e), y, xs(d)) for e in (1, -1) for d in range(NX)]
    for peer in peers:
        pl.semaphore_signal(barrier, inc=1, device_id=peer, device_id_type=MESH)

    load_w.wait()
    w_rows = wloc.shape[0]
    lane_w = lax.broadcasted_iota(jnp.int32, (w_rows, 128), 1)
    q_width = HEADS * HEAD_DIM
    g_width = GROUP * HEAD_DIM
    for t in range(NX):
        k_tile = wloc[:, q_width + 128 * (t // 2) : q_width + 128 * (t // 2) + 128]
        v_at = q_width + KV_HEADS * HEAD_DIM + 128 * (t // 2)
        v_tile = wloc[:, v_at : v_at + 128]
        k_tile = k_tile.astype(jnp.float32)
        v_tile = v_tile.astype(jnp.float32)
        if t % 2 == 0:
            v_tile = pltpu.roll(v_tile, 64, 1)
        else:
            k_tile = pltpu.roll(k_tile, 64, 1)
        wsp[t, :, :g_width] = wloc[:, g_width * t : g_width * (t + 1)]
        wsp[t, :, g_width:] = jnp.where(lane_w < 64, k_tile, v_tile).astype(jnp.bfloat16)
    wi[y, x // 2, lax.rem(x, 2)] = wsp[x]
    load_x.wait()
    pl.semaphore_wait(barrier, len(peers))

    def place(buf, yy, xx):
        return buf.at[yy, xx // 2, lax.rem(xx, 2)]

    wi_in = [
        send(wsp.at[xs(d)], place(wi, y, x), (p, y, xs(d)), place(wi, y, xs(-d)))
        for d in (1, -1, 2)
    ]
    first, second = pl.ds(0, half), pl.ds(half, half)
    up, down = (p, y, xs(1)), (p, y, xs(-1))
    x_up_a = send(xg.at[0, first], xg.at[1, first], up)
    x_down_b = send(xg.at[0, second], xg.at[2, second], down)
    x_up_b = send(xg.at[0, second], xg.at[1, second], up)
    x_down_a = send(xg.at[0, first], xg.at[2, first], down)

    north, south = (p, ys(1), x), (p, ys(-1), x)
    reach = n_y // 2

    def ring_send(buf, step):
        arrivals = []
        order = ((0, 1), (1, -1), (1, 1), (0, -1))
        for u, way in order:
            if step == reach - 1 and (u, way) not in ((0, 1), (1, -1)):
                continue
            piece = buf.at[ys(-way * step), u]
            landing = buf.at[ys(-way * (step + 1)), u]
            arrivals.append((u, way, piece, landing))
        return arrivals

    def ring_start(buf):
        return [
            send(piece, piece, north if way == 1 else south, landing)
            for u, way, piece, landing in ring_send(buf, 0)
        ]

    def ring_step(buf, step, arrivals):
        following = {(u, way): (piece, landing) for u, way, piece, landing in (
            ring_send(buf, step + 1) if step + 1 < reach else []
        )}
        result = []
        for (u, way, _, _), arrive in zip(ring_send(buf, step), arrivals):
            arrive()
            if (u, way) in following:
                piece, landing = following[(u, way)]
                result.append(send(piece, piece, north if way == 1 else south, landing))
        return result

    for arrive in wi_in:
        arrive()
    wi_ring = ring_start(wi)

    ends = []
    total = 0
    for i in range(lengths.shape[1]):
        total = total + lengths[p, i]
        ends.append(total)
    deltas = (0, -1, 1, 2)
    lane = lax.broadcasted_iota(jnp.int32, (rows, 128), 1)
    row = lax.broadcasted_iota(jnp.int32, (rows, 128), 0)

    def make_trig(slot):
        spots = y * span + xs(deltas[slot]) * rows + row
        place_in = (spots - response_start(ends, spots)).astype(jnp.float32)
        sine, cosine = sine_cosine(place_in * inverse[...])
        trig[slot, 0] = cosine
        trig[slot, 1] = jnp.where((lane & 63) < 32, -sine, sine)

    norm_rows = 16

    def normalize(slot):
        def step(i, carry):
            at = pl.ds(pl.multiple_of(i * norm_rows, norm_rows), norm_rows)
            wide = xg[slot, at, :].astype(jnp.float32)
            scale = lax.rsqrt(jnp.mean(wide * wide, -1, keepdims=True) + epsilon)
            to = pl.ds(pl.multiple_of(slot * rows + i * norm_rows, norm_rows), norm_rows)
            xn[to, :] = (wide * scale * gain[...]).astype(jnp.bfloat16)
            return carry

        lax.fori_loop(0, rows // norm_rows, step, 0)

    for slot in range(4):
        make_trig(slot)
    normalize(0)

    wi_ring = ring_step(wi, 0, wi_ring)
    x_up_a()
    x_far_a = send(xg.at[1, first], xg.at[3, first], up)
    x_down_b()
    x_far_b = send(xg.at[2, second], xg.at[3, second], down)
    wo_in = []
    for d in (1, -1, 2):
        cols = pl.ds(pl.multiple_of(xs(d) * out_cols, out_cols), out_cols)
        wo_in.append(
            send(wo_hbm.at[:, cols], place(wo, y, x), (p, y, xs(d)), place(wo, y, xs(-d)))
        )
    for step in range(1, reach - 1):
        wi_ring = ring_step(wi, step, wi_ring)
    x_up_b()
    normalize(1)
    x_down_a()
    normalize(2)
    load_o.wait()
    for arrive in wo_in:
        arrive()
    wo_ring = ring_start(wo)
    wi_ring = ring_step(wi, reach - 1, wi_ring)

    def project(slot, count):
        proj = jnp.dot(
            xn[slot * rows : (slot + count) * rows, :],
            wi[...].reshape(depth, COLS),
            preferred_element_type=jnp.float32,
        )
        arrivals = []
        for i in range(count):
            own = proj[i * rows : (i + 1) * rows]
            cosine, sine = trig[slot + i, 0], trig[slot + i, 1]
            block = xs(deltas[slot + i])

            def rotated(tile):
                partner = jnp.where(
                    (lane & 63) < 32, pltpu.roll(tile, 96, 1), pltpu.roll(tile, 32, 1)
                )
                return tile * cosine + partner * sine

            tail = own[:, g_width:]
            kv[2 * NX + block] = jnp.where(lane < 64, rotated(tail), tail).astype(jnp.bfloat16)
            arrivals.append(
                send(kv.at[2 * NX + block], kv.at[NX + block], north)
            )
            for t in range(GROUP // 2):
                tile = rotated(own[:, 128 * t : 128 * (t + 1)]) * HEAD_DIM**-0.5
                q_s[block, 2 * t] = jnp.where(lane < 64, tile, 0.0).astype(jnp.bfloat16)
                q_s[block, 2 * t + 1] = jnp.where(
                    lane < 64, pltpu.roll(tile, 64, 1), 0.0
                ).astype(jnp.bfloat16)
        return arrivals

    near = project(0, 3)
    x_far_a()
    x_far_b()
    normalize(3)
    near += project(3, 1)
    wo_ring = ring_step(wo, 0, wo_ring)
    far = []
    for slot in range(4):
        near[slot]()
        block = xs(deltas[slot])
        far.append(send(kv.at[NX + block], kv.at[block], north))
    for step in range(1, reach - 1):
        wo_ring = ring_step(wo, step, wo_ring)
    for arrive in far:
        arrive()

    lane_p = lax.broadcasted_iota(jnp.int32, (part, 128), 1)
    row_p = lax.broadcasted_iota(jnp.int32, (part, 128), 0)

    def attend(i):
        def one(j, carry):
            queries = q_s[j, :, i * part : (i + 1) * part, :].reshape(GROUP * part, 128)
            window = kv[pl.ds(j, WINDOW)].reshape(WINDOW * rows, 128)
            scores = lax.dot_general(
                queries, window, (((1,), (1,)), ((), ())), preferred_element_type=jnp.float32
            )
            spots = y * span + j * rows + i * part + row_p
            start = response_start(ends, spots)
            allowed = []
            for c in range(WINDOW):
                keys = y * span + (j + c - 2 * NX) * rows + lane_p
                allowed.append((keys >= start) & (keys <= spots))
            allowed = jnp.concatenate(allowed, 1)
            scores = jnp.where(
                allowed[None], scores.reshape(GROUP, part, WINDOW * rows), masked_score
            )
            probs = jnp.exp(scores - jnp.max(scores, -1, keepdims=True))
            denom = jnp.sum(probs, -1, keepdims=True)
            mixed = jnp.dot(
                probs.astype(jnp.bfloat16).reshape(GROUP * part, WINDOW * rows),
                window,
                preferred_element_type=jnp.float32,
            ).reshape(GROUP, part, 128)
            mixed = mixed / denom
            tiles = [
                jnp.where(lane_p < 64, pltpu.roll(mixed[2 * t], 64, 1), mixed[2 * t + 1])
                for t in range(GROUP // 2)
            ]
            att[i, x, j] = jnp.concatenate(tiles, 1).astype(jnp.bfloat16)
            return carry

        lax.fori_loop(0, NX, one, 0)

    low, high = pl.ds(0, NX // 2), pl.ds(NX // 2, NX // 2)

    def att_start(i):
        return (
            send(att.at[i, x, low], att.at[i, x, low], up, att.at[i, xs(-1), low]),
            send(att.at[i, x, high], att.at[i, x, high], down, att.at[i, xs(1), high]),
            send(att.at[i, x, high], att.at[i, x, high], up, att.at[i, xs(-1), high]),
            send(att.at[i, x, low], att.at[i, x, low], down, att.at[i, xs(1), low]),
        )

    def att_pass(i, arrivals):
        arrivals[0]()
        piece = att.at[i, xs(-1), low]
        far_low = send(piece, piece, up, att.at[i, xs(2), low])
        arrivals[1]()
        piece = att.at[i, xs(1), high]
        far_high = send(piece, piece, down, att.at[i, xs(2), high])
        return (arrivals[2], arrivals[3], far_low, far_high)

    def finish(i):
        weight = wo[...].reshape(q_width, out_cols)
        result = None
        for h in range(NX):
            term = jnp.dot(
                att[i, h].reshape(NX * part, g_width),
                weight[h * g_width : (h + 1) * g_width],
                preferred_element_type=jnp.float32,
            )
            result = term if result is None else result + term
        acc[...] = result
        arrivals = []
        for slot in (3, 2, 1, 0):
            d = deltas[slot]
            j = xs(d)
            kept = xg[slot, i * part : (i + 1) * part, own_cols].astype(jnp.float32)
            at = pl.ds(pl.multiple_of(j * part, part), part)
            obuf[i, slot] = (acc[at, :] + kept).astype(jnp.bfloat16)
            from_cols = pl.ds(pl.multiple_of(xs(-d) * out_cols, out_cols), out_cols)
            there = pl.ds(i * part, part)
            arrivals.append(
                send(
                    obuf.at[i, slot],
                    out.at[there, own_cols],
                    (ps(1), y, j),
                    out.at[there, from_cols],
                )
            )
        return arrivals

    attend(0)
    arrivals_0 = att_start(0)
    wo_ring = ring_step(wo, reach - 1, wo_ring)
    attend(1)
    arrivals_1 = att_start(1)
    arrivals_0 = att_pass(0, arrivals_0)
    for arrive in arrivals_0:
        arrive()
    last = finish(0)
    for arrive in att_pass(1, arrivals_1):
        arrive()
    last += finish(1)
    for arrive in last:
        arrive()
    for copy in pending:
        copy.wait_send()


def body(states, norm_gain, w_in, w_out, lengths):
    rows, depth = states.shape[1:]
    w_rows = w_in.shape[1]
    o_rows = w_out.shape[1]
    out_cols = depth // NX
    n_pipe = lax.axis_size("pipe")
    n_y = lax.axis_size("ctx_y")
    part = rows // CHUNKS
    copies = 128
    half_dim = HEAD_DIM // 2
    inverse = rope_base ** (-jnp.arange(half_dim, dtype=jnp.float32) * 2.0 / HEAD_DIM)
    inverse = jnp.tile(inverse, 128 // half_dim)[None, :]
    bf16, f32 = jnp.bfloat16, jnp.float32
    moved = pl.pallas_call(
        functools.partial(tick_kernel, n_pipe, n_y),
        out_shape=jax.ShapeDtypeStruct((rows, depth), bf16),
        in_specs=[
            pl.BlockSpec(memory_space=pltpu.SMEM),
            pl.BlockSpec(memory_space=pltpu.VMEM),
            pl.BlockSpec(memory_space=pltpu.VMEM),
            pl.BlockSpec(memory_space=pl.ANY),
            pl.BlockSpec(memory_space=pl.ANY),
            pl.BlockSpec(memory_space=pl.ANY),
        ],
        out_specs=pl.BlockSpec(memory_space=pl.ANY),
        scratch_shapes=[
            pltpu.VMEM((4, rows, depth), bf16),
            pltpu.VMEM((4 * rows, depth), bf16),
            pltpu.VMEM((w_rows, w_in.shape[2]), bf16),
            pltpu.VMEM((NX, w_rows, COLS), bf16),
            pltpu.VMEM((n_y, 2, 2, w_rows, COLS), bf16),
            pltpu.VMEM((n_y, 2, 2, o_rows, out_cols), bf16),
            pltpu.VMEM((4, 2, rows, 128), f32),
            pltpu.VMEM((NX, GROUP, rows, 128), bf16),
            pltpu.VMEM((3 * NX, rows, 128), bf16),
            pltpu.VMEM((CHUNKS, NX, NX, part, GROUP * HEAD_DIM), bf16),
            pltpu.VMEM((NX * part, out_cols), f32),
            pltpu.VMEM((CHUNKS, 4, part, out_cols), bf16),
            pltpu.SemaphoreType.DMA((3,)),
            pltpu.SemaphoreType.DMA((copies,)),
            pltpu.SemaphoreType.DMA((copies,)),
        ],
        compiler_params=pltpu.CompilerParams(
            collective_id=0, has_side_effects=True, vmem_limit_bytes=60 * 1024 * 1024
        ),
        name="tick",
    )(lengths, inverse, norm_gain, states[0], w_in[0], w_out[0])
    return moved[None]


def solution(mesh):
    n_pipe = mesh.shape["pipe"]
    n_y = mesh.shape["ctx"] // NX
    finer = Mesh(mesh.devices.reshape(n_pipe, n_y, NX), ("pipe", "ctx_y", "ctx_x"))
    ctx = ("ctx_y", "ctx_x")
    placed = (
        P("pipe", ctx, None),
        P("pipe", None),
        P("pipe", ctx, None),
        P("pipe", ctx, None),
        P(),
    )
    return jax.shard_map(
        body, mesh=finer, in_specs=placed, out_specs=P("pipe", ctx, None), check_vma=False
    )
```

time: 208 us -> 80.8 us (0.39)
  the two profiles are of different devices: /device:TPU:40 before, /device:TPU:1 now
where the time goes in v1:
time: 80.8 us; the launch traced here: 80.6 us
  Pallas kernels  77.3 us (96%)
  local copies, waits for them, and re-layouts  3.22 us (4%)
    pallas_call x1, Pallas kernels, body(): pl.pallas_call(functools.partial(tick_kernel, n_pipe, n_y), out_shape=jax...  77.3 us
    unnamed x4, local copies, waits for them, and re-layouts  2.63 us

profile of v1, /device:TPU:1, one launch (start us, length us, event | category | flops | bytes accessed | tf_op | source)
XLA Modules:
  0.0 80.6 jit_solution(10200096702274327313)
XLA Ops:
  0.0 0.0 copy-start
  0.0 0.6 broadcast_in_dim_tile.3.inverse
  0.6 0.1 copy-done
  0.7 0.7 copy.6.lengths
  1.4 77.3 %tick.1 = bf16[128,2048]{1,0:T(8,128)(2,1)} custom-call(s32[16,8]{1,0:T(8,128)} %copy.6.lengths, f32[1,128]{1,0:T(1,128)} %broadcast_in_dim_tile.3.inverse, f32[1,2048]{1,0:T(1,128)} %gain.1, bf16[128,2048]{1,0:T(8,128)(2,1)} %bitcast.5, bf16[64,1536]{1,0:T(8,128)(2,1)} %bitcast.6, bf16[32,2048]{1,0:T(8,128)(2,1)} %bitcast.7), custom_call_target="tpu_custom_call" | custom-call | tf_op jit(solution)/shard_map/tick/pallas_call | solution.py:435
  78.7 1.9 %copy.8 = bf16[1,128,2048]{2,1,0:T(8,128)(2,1)} copy(bf16[1,128,2048]{2,1,0:T(8,128)(2,1)} %bitcast.4) | data formatting | bytes 1048576
  (2 shorter events, 0.0 us)
Async XLA Ops:
  0.0 0.7 copy-start

commit v2 on v1

v2 whole, which is shorter than its diff:
```python
import functools
import math

import jax
import jax.numpy as jnp
from jax import lax
from jax.experimental import pallas as pl
from jax.experimental.pallas import tpu as pltpu
from jax.sharding import Mesh
from jax.sharding import PartitionSpec as P

HEAD_DIM = 64
HEADS = 16
KV_HEADS = 4
GROUP = HEADS // KV_HEADS
NX = 4
CHUNKS = 2
WINDOW = 9
COLS = (GROUP + 2) * HEAD_DIM

epsilon = 1e-05
rope_base = 500000.0
masked_score = -1e30
MESH = pl.DeviceIdType.MESH


def sine_cosine(angle):
    turns = jnp.floor(angle * (2.0 / math.pi) + 0.5)
    quarter = turns.astype(jnp.int32)
    rest = angle - turns * 1.5703125
    rest = rest - turns * 4.837512969970703125e-4
    rest = rest - turns * 7.54978995489188216e-8
    z = rest * rest
    sine = ((-1.9515295891e-4 * z + 8.3321608736e-3) * z - 1.6666654611e-1) * z * rest + rest
    cosine = (
        (2.443315711809948e-5 * z - 1.388731625493765e-3) * z + 4.166664568298827e-2
    ) * z * z - 0.5 * z + 1.0
    odd = (quarter & 1) == 1
    sine, cosine = jnp.where(odd, cosine, sine), jnp.where(odd, sine, cosine)
    sine = jnp.where((quarter & 2) == 2, -sine, sine)
    cosine = jnp.where(((quarter + 1) & 2) == 2, -cosine, cosine)
    return sine, cosine


def response_start(ends, spots):
    start = jnp.zeros_like(spots)
    for end in ends:
        start = jnp.maximum(start, jnp.where(spots >= end, end, 0))
    return start


def tick_kernel(
    n_pipe,
    n_y,
    lengths_hbm,
    gain_hbm,
    x_hbm,
    wi_hbm,
    wo_hbm,
    out,
    lengths,
    gain,
    xg,
    xn,
    wloc,
    wsp,
    wi,
    wo,
    trig,
    q_s,
    kv,
    v_one,
    att,
    acc,
    obuf,
    local_sem,
    send_sem,
    recv_sem,
):
    p = lax.axis_index("pipe")
    y = lax.axis_index("ctx_y")
    x = lax.axis_index("ctx_x")
    rows = xg.shape[1]
    half = rows // 2
    part = rows // CHUNKS
    depth = xg.shape[2]
    out_cols = acc.shape[1]
    span = NX * rows

    def xs(d):
        return lax.rem(x + (d + NX), NX)

    def ys(d):
        return lax.rem(y + (d + n_y), n_y)

    def ps(d):
        return lax.rem(p + (d + n_pipe), n_pipe)

    counter = [0]
    pending = []

    def send(src, dst, device, landing=None):
        k = counter[0]
        counter[0] += 1
        copy = pltpu.make_async_remote_copy(
            src_ref=src,
            dst_ref=dst,
            send_sem=send_sem.at[k],
            recv_sem=recv_sem.at[k],
            device_id=device,
            device_id_type=MESH,
        )
        copy.start()
        pending.append(copy)
        land = dst if landing is None else landing

        def arrive():
            pltpu.make_async_remote_copy(
                src_ref=land,
                dst_ref=land,
                send_sem=send_sem.at[k],
                recv_sem=recv_sem.at[k],
                device_id=device,
                device_id_type=MESH,
            ).wait_recv()

        return arrive

    load_w = pltpu.make_async_copy(wi_hbm, wloc, local_sem.at[0])
    load_x = pltpu.make_async_copy(x_hbm, xg.at[0], local_sem.at[1])
    own_cols = pl.ds(pl.multiple_of(x * out_cols, out_cols), out_cols)
    load_o = pltpu.make_async_copy(
        wo_hbm.at[:, own_cols], wo.at[y, x // 2, lax.rem(x, 2)], local_sem.at[2]
    )
    load_g = pltpu.make_async_copy(gain_hbm, gain, local_sem.at[3])
    load_l = pltpu.make_async_copy(lengths_hbm, lengths, local_sem.at[4])
    load_w.start()
    load_x.start()

    barrier = pltpu.get_barrier_semaphore()
    peers = [(p, y, xs(d)) for d in (1, 2, 3)]
    peers += [(p, ys(d), x) for d in (1, -1)]
    peers += [(ps(e), y, xs(d)) for e in (1, -1) for d in range(NX)]
    for peer in peers:
        pl.semaphore_signal(barrier, inc=1, device_id=peer, device_id_type=MESH)
    load_l.start()
    load_g.start()
    load_o.start()

    load_w.wait()
    w_rows = wloc.shape[0]
    lane_w = lax.broadcasted_iota(jnp.int32, (w_rows, 128), 1)
    q_width = HEADS * HEAD_DIM
    g_width = GROUP * HEAD_DIM
    for t in range(NX):
        k_tile = wloc[:, q_width + 128 * (t // 2) : q_width + 128 * (t // 2) + 128]
        v_at = q_width + KV_HEADS * HEAD_DIM + 128 * (t // 2)
        v_tile = wloc[:, v_at : v_at + 128]
        k_tile = k_tile.astype(jnp.float32)
        v_tile = v_tile.astype(jnp.float32)
        if t % 2 == 0:
            v_tile = pltpu.roll(v_tile, 64, 1)
        else:
            k_tile = pltpu.roll(k_tile, 64, 1)
        wsp[t, :, :g_width] = wloc[:, g_width * t : g_width * (t + 1)]
        wsp[t, :, g_width:] = jnp.where(lane_w < 64, k_tile, v_tile).astype(jnp.bfloat16)
    wi[y, x] = wsp[x]
    load_x.wait()
    with jax.named_scope("barrier"):
        pl.semaphore_wait(barrier, len(peers))

    def place(buf, yy, xx):
        return buf.at[yy, xx // 2, lax.rem(xx, 2)]

    north, south = (p, ys(1), x), (p, ys(-1), x)
    toward = {1: north, -1: south}
    reach = n_y // 2

    def piece_wi(dy, d):
        return wi.at[ys(dy), xs(d)]

    def piece_wo(dy, u):
        return wo.at[ys(dy), u]

    wi_order = ((0, 1), (0, -1), (-1, 1), (1, -1), (1, 1), (-1, -1), (2, 1), (2, -1))
    wi_final = ((0, 1), (1, -1), (-1, 1), (2, -1))
    wo_order = ((0, 1), (1, -1), (1, 1), (0, -1))
    wo_final = ((0, 1), (1, -1))

    def ring_send(piece, u, way, step):
        source = piece(-way * step, u)
        return send(source, source, toward[way], piece(-way * (step + 1), u))

    def ring_step(piece, order, final, step, arrivals):
        result = {}
        for key in order:
            if key not in arrivals:
                continue
            arrivals[key]()
            if step + 1 < reach - 1 or (step + 1 == reach - 1 and key in final):
                result[key] = ring_send(piece, key[0], key[1], step + 1)
        return result

    wi_ring = {(0, way): ring_send(piece_wi, 0, way, 0) for way in (1, -1)}
    wi_in = {
        -d: send(wsp.at[xs(d)], piece_wi(0, 0), (p, y, xs(d)), piece_wi(0, -d))
        for d in (1, -1)
    }
    wi_in[2] = send(wsp.at[xs(2)], piece_wi(0, 0), (p, y, xs(2)), piece_wi(0, 2))
    first, second = pl.ds(0, half), pl.ds(half, half)
    up, down = (p, y, xs(1)), (p, y, xs(-1))
    x_up_a = send(xg.at[0, first], xg.at[1, first], up)
    x_down_b = send(xg.at[0, second], xg.at[2, second], down)
    x_up_b = send(xg.at[0, second], xg.at[1, second], up)
    x_down_a = send(xg.at[0, first], xg.at[2, first], down)
    for d in (-1, 1, 2):
        with jax.named_scope(f"wi_in{d}"):
            wi_in[d]()
        for way in (1, -1):
            wi_ring[d, way] = ring_send(piece_wi, d, way, 0)

    load_l.wait()
    load_g.wait()
    ends = []
    total = 0
    for i in range(lengths.shape[0]):
        total = total + lengths[i, p]
        ends.append(total)
    deltas = (0, -1, 1, 2)
    lane = lax.broadcasted_iota(jnp.int32, (rows, 128), 1)
    row = lax.broadcasted_iota(jnp.int32, (rows, 128), 0)
    half_dim = HEAD_DIM // 2
    turn = lax.broadcasted_iota(jnp.int32, (8, 128), 1) & (half_dim - 1)
    inverse = jnp.zeros((8, 128), jnp.float32)
    for i in range(half_dim):
        inverse = jnp.where(turn == i, rope_base ** (-2.0 * i / HEAD_DIM), inverse)

    def make_trig(slot):
        spots = y * span + xs(deltas[slot]) * rows + row
        place_in = (spots - response_start(ends, spots)).astype(jnp.float32)
        sine, cosine = sine_cosine(place_in * inverse[:1])
        trig[slot, 0] = cosine
        trig[slot, 1] = jnp.where((lane & 63) < 32, -sine, sine)

    norm_rows = 32

    def normalize(slot):
        def step(i, carry):
            at = pl.ds(pl.multiple_of(i * norm_rows, norm_rows), norm_rows)
            wide = xg[slot, at, :].astype(jnp.float32)
            scale = lax.rsqrt(jnp.mean(wide * wide, -1, keepdims=True) + epsilon)
            to = pl.ds(pl.multiple_of(slot * rows + i * norm_rows, norm_rows), norm_rows)
            xn[to, :] = (wide * scale * gain[...]).astype(jnp.bfloat16)
            return carry

        lax.fori_loop(0, rows // norm_rows, step, 0, unroll=2)

    with jax.named_scope("trig"):
        for slot in range(4):
            make_trig(slot)
    with jax.named_scope("norm0"):
        normalize(0)

    with jax.named_scope("ring0"):
        wi_ring = ring_step(piece_wi, wi_order, wi_final, 0, wi_ring)
    with jax.named_scope("x_first"):
        x_up_a()
        x_far_a = send(xg.at[1, first], xg.at[3, first], up)
        x_down_b()
        x_far_b = send(xg.at[2, second], xg.at[3, second], down)
    wo_in = []
    for d in (1, -1, 2):
        cols = pl.ds(pl.multiple_of(xs(d) * out_cols, out_cols), out_cols)
        wo_in.append(
            send(wo_hbm.at[:, cols], place(wo, y, x), (p, y, xs(d)), place(wo, y, xs(-d)))
        )
    with jax.named_scope("ring12"):
        for step in range(1, reach - 1):
            wi_ring = ring_step(piece_wi, wi_order, wi_final, step, wi_ring)
    with jax.named_scope("x_second"):
        x_up_b()
        x_down_a()
    with jax.named_scope("norm12"):
        normalize(1)
        normalize(2)
    with jax.named_scope("ring3"):
        wi_ring = ring_step(piece_wi, wi_order, wi_final, reach - 1, wi_ring)

    def rotated(tile, slot):
        partner = jnp.where((lane & 63) < 32, pltpu.roll(tile, 96, 1), pltpu.roll(tile, 32, 1))
        return tile * trig[slot, 0] + partner * trig[slot, 1]

    def project(slot, count, first_col, last_col):
        return jnp.dot(
            xn[slot * rows : (slot + count) * rows, :],
            wi[:, :, :, first_col:last_col].reshape(depth, last_col - first_col),
            preferred_element_type=jnp.float32,
        )

    def project_kv(slot, count):
        proj = project(slot, count, g_width, COLS)
        arrivals = []
        for i in range(count):
            own = proj[i * rows : (i + 1) * rows]
            block = xs(deltas[slot + i])
            own = jnp.where(lane < 64, rotated(own, slot + i), own)
            kv[2 * NX + block] = own.astype(jnp.bfloat16)
            arrivals.append(send(kv.at[2 * NX + block], kv.at[NX + block], north))
        return arrivals

    def project_q(slot, count):
        proj = project(slot, count, 0, g_width)
        for i in range(count):
            own = proj[i * rows : (i + 1) * rows]
            block = xs(deltas[slot + i])
            for t in range(GROUP // 2):
                tile = rotated(own[:, 128 * t : 128 * (t + 1)], slot + i) * HEAD_DIM**-0.5
                q_s[block, 2 * t] = jnp.where(lane < 64, tile, 0.0).astype(jnp.bfloat16)
                q_s[block, 2 * t + 1] = jnp.where(
                    lane < 64, pltpu.roll(tile, 64, 1), 0.0
                ).astype(jnp.bfloat16)

    with jax.named_scope("kv012"):
        near = project_kv(0, 3)
    with jax.named_scope("x_far"):
        x_far_a()
        x_far_b()
    with jax.named_scope("norm3"):
        normalize(3)
    with jax.named_scope("kv3"):
        near += project_kv(3, 1)
    block = xs(deltas[3])
    far = [send(kv.at[2 * NX + block], kv.at[block], (p, ys(2), x))]
    with jax.named_scope("wo_in"):
        load_o.wait()
        for arrive in wo_in:
            arrive()
    wo_ring = {key: ring_send(piece_wo, *key, 0) for key in wo_order if key[1] == -1}
    with jax.named_scope("q012"):
        project_q(0, 3)
    with jax.named_scope("kv_near"):
        for slot in range(3):
            near[slot]()
            block = xs(deltas[slot])
            far.append(send(kv.at[NX + block], kv.at[block], north))
    wo_ring.update({key: ring_send(piece_wo, *key, 0) for key in wo_order if key[1] == 1})
    with jax.named_scope("q3"):
        project_q(3, 1)
    with jax.named_scope("kv_far"):
        near[3]()
        for arrive in far:
            arrive()
    with jax.named_scope("v_one"):
        for b in range(3 * NX):
            v_one[b] = jnp.where(lane < 64, 1.0, kv[b].astype(jnp.float32)).astype(jnp.bfloat16)

    lane_p = lax.broadcasted_iota(jnp.int32, (part, 128), 1)
    row_p = lax.broadcasted_iota(jnp.int32, (part, 128), 0)

    def attend(i, j):
        queries = q_s[j, :, i * part : (i + 1) * part, :].reshape(GROUP * part, 128)
        window = kv[j : j + WINDOW].reshape(WINDOW * rows, 128)
        values = v_one[j : j + WINDOW].reshape(WINDOW * rows, 128)
        scores = lax.dot_general(
            queries, window, (((1,), (1,)), ((), ())), preferred_element_type=jnp.float32
        )
        spots = y * span + j * rows + i * part + row_p
        start = response_start(ends, spots)
        allowed = []
        for c in range(WINDOW):
            keys = y * span + (j + c - 2 * NX) * rows + lane_p
            inside = keys >= start
            if c == WINDOW - 1:
                inside = inside & (keys <= spots)
            allowed.append(inside)
        allowed = jnp.concatenate(allowed, 1)
        scores = jnp.where(
            allowed[None], scores.reshape(GROUP, part, WINDOW * rows), masked_score
        )
        probs = jnp.exp(scores - jnp.max(scores, -1, keepdims=True))
        mixed = jnp.dot(
            probs.astype(jnp.bfloat16).reshape(GROUP * part, WINDOW * rows),
            values,
            preferred_element_type=jnp.float32,
        )
        turned = pltpu.roll(mixed, 64, 1)
        tiles = []
        for t in range(GROUP // 2):
            even = slice(2 * t * part, (2 * t + 1) * part)
            odd = slice((2 * t + 1) * part, (2 * t + 2) * part)
            tiles.append(
                jnp.where(lane_p < 64, turned[even] / mixed[even], mixed[odd] / turned[odd])
            )
        att[i, x, j] = jnp.concatenate(tiles, 1).astype(jnp.bfloat16)

    low, high = pl.ds(0, NX // 2), pl.ds(NX // 2, NX // 2)

    def att_start(i):
        return (
            send(att.at[i, x, low], att.at[i, x, low], up, att.at[i, xs(-1), low]),
            send(att.at[i, x, high], att.at[i, x, high], down, att.at[i, xs(1), high]),
            send(att.at[i, x, high], att.at[i, x, high], up, att.at[i, xs(-1), high]),
            send(att.at[i, x, low], att.at[i, x, low], down, att.at[i, xs(1), low]),
        )

    def att_pass(i, arrivals):
        arrivals[0]()
        piece = att.at[i, xs(-1), low]
        far_low = send(piece, piece, up, att.at[i, xs(2), low])
        arrivals[1]()
        piece = att.at[i, xs(1), high]
        far_high = send(piece, piece, down, att.at[i, xs(2), high])
        return (arrivals[2], arrivals[3], far_low, far_high)

    def finish(i):
        weight = wo[...].reshape(q_width, out_cols)
        result = None
        for h in range(NX):
            term = jnp.dot(
                att[i, h].reshape(NX * part, g_width),
                weight[h * g_width : (h + 1) * g_width],
                preferred_element_type=jnp.float32,
            )
            result = term if result is None else result + term
        acc[...] = result
        arrivals = []
        for slot in (3, 2, 1, 0):
            d = deltas[slot]
            j = xs(d)
            kept = xg[slot, i * part : (i + 1) * part, own_cols].astype(jnp.float32)
            at = pl.ds(pl.multiple_of(j * part, part), part)
            obuf[i, slot] = (acc[at, :] + kept).astype(jnp.bfloat16)
            from_cols = pl.ds(pl.multiple_of(xs(-d) * out_cols, out_cols), out_cols)
            there = pl.ds(i * part, part)
            arrivals.append(
                send(
                    obuf.at[i, slot],
                    out.at[there, own_cols],
                    (ps(1), y, j),
                    out.at[there, from_cols],
                )
            )
        return arrivals

    with jax.named_scope("attend0a"):
        attend(0, 0)
        attend(0, 1)
    with jax.named_scope("wo0"):
        wo_ring = ring_step(piece_wo, wo_order, wo_final, 0, wo_ring)
    with jax.named_scope("attend0b"):
        attend(0, 2)
        attend(0, 3)
    arrivals_0 = att_start(0)
    with jax.named_scope("attend1a"):
        attend(1, 0)
        attend(1, 1)
    for step in range(1, reach - 2):
        with jax.named_scope("wo1"):
            wo_ring = ring_step(piece_wo, wo_order, wo_final, step, wo_ring)
    with jax.named_scope("attend1b"):
        attend(1, 2)
        attend(1, 3)
    with jax.named_scope("pass0"):
        arrivals_0 = att_pass(0, arrivals_0)
    arrivals_1 = att_start(1)
    with jax.named_scope("wo2"):
        if reach > 2:
            wo_ring = ring_step(piece_wo, wo_order, wo_final, reach - 2, wo_ring)
    with jax.named_scope("att0_in"):
        for arrive in arrivals_0:
            arrive()
    with jax.named_scope("pass1"):
        arrivals_1 = att_pass(1, arrivals_1)
    with jax.named_scope("wo3"):
        wo_ring = ring_step(piece_wo, wo_order, wo_final, reach - 1, wo_ring)
    with jax.named_scope("finish0"):
        last = finish(0)
    with jax.named_scope("att1_in"):
        for arrive in arrivals_1:
            arrive()
    with jax.named_scope("finish1"):
        last += finish(1)
    with jax.named_scope("out_in"):
        for arrive in last:
            arrive()
    with jax.named_scope("wait_send"):
        for copy in pending:
            copy.wait_send()


def body(states, norm_gain, w_in, w_out, lengths):
    rows, depth = states.shape[1:]
    w_rows = w_in.shape[1]
    o_rows = w_out.shape[1]
    out_cols = depth // NX
    n_pipe = lax.axis_size("pipe")
    n_y = lax.axis_size("ctx_y")
    part = rows // CHUNKS
    copies = 128
    bf16, f32 = jnp.bfloat16, jnp.float32
    moved = pl.pallas_call(
        functools.partial(tick_kernel, n_pipe, n_y),
        out_shape=pltpu.VMEM((rows, depth), bf16),
        in_specs=[
            pl.BlockSpec(memory_space=pl.ANY),
            pl.BlockSpec(memory_space=pl.ANY),
            pl.BlockSpec(memory_space=pl.ANY),
            pl.BlockSpec(memory_space=pl.ANY),
            pl.BlockSpec(memory_space=pl.ANY),
        ],
        out_specs=pl.BlockSpec(memory_space=pltpu.VMEM),
        scratch_shapes=[
            pltpu.SMEM(lengths.shape[::-1], jnp.int32),
            pltpu.VMEM((1, depth), f32),
            pltpu.VMEM((4, rows, depth), bf16),
            pltpu.VMEM((4 * rows, depth), bf16),
            pltpu.VMEM((w_rows, w_in.shape[2]), bf16),
            pltpu.VMEM((NX, w_rows, COLS), bf16),
            pltpu.VMEM((n_y, NX, w_rows, COLS), bf16),
            pltpu.VMEM((n_y, 2, 2, o_rows, out_cols), bf16),
            pltpu.VMEM((4, 2, rows, 128), f32),
            pltpu.VMEM((NX, GROUP, rows, 128), bf16),
            pltpu.VMEM((3 * NX, rows, 128), bf16),
            pltpu.VMEM((3 * NX, rows, 128), bf16),
            pltpu.VMEM((CHUNKS, NX, NX, part, GROUP * HEAD_DIM), bf16),
            pltpu.VMEM((NX * part, out_cols), f32),
            pltpu.VMEM((CHUNKS, 4, part, out_cols), bf16),
            pltpu.SemaphoreType.DMA((5,)),
            pltpu.SemaphoreType.DMA((copies,)),
            pltpu.SemaphoreType.DMA((copies,)),
        ],
        compiler_params=pltpu.CompilerParams(
            collective_id=0, has_side_effects=True, vmem_limit_bytes=60 * 1024 * 1024
        ),
        name="tick",
    )(lengths.T, norm_gain, states[0], w_in[0], w_out[0])
    return moved[None]


def solution(mesh):
    n_pipe = mesh.shape["pipe"]
    n_y = mesh.shape["ctx"] // NX
    finer = Mesh(mesh.devices.reshape(n_pipe, n_y, NX), ("pipe", "ctx_y", "ctx_x"))
    ctx = ("ctx_y", "ctx_x")
    placed = (
        P("pipe", ctx, None),
        P("pipe", None),
        P("pipe", ctx, None),
        P("pipe", ctx, None),
        P(),
    )
    return jax.shard_map(
        body, mesh=finer, in_specs=placed, out_specs=P("pipe", ctx, None), check_vma=False
    )
```

time: 80.8 us -> 69.8 us (0.86)
  Pallas kernels: 77.3 us -> 68.9 us
  local copies, waits for them, and re-layouts: 3.22 us -> 0.8 us
    pallas_call x1, Pallas kernels: 77.3 us -> 68.9 us  [body(): pl.pallas_call(functools.partial(tick_kernel, n_pipe, n_y), out_shape=plt...]
    unnamed x4 -> x1, local copies, waits for them, and re-layouts: 2.63 us -> 0.8 us
where the time goes in v2:
time: 69.8 us; the launch traced here: 69.7 us
  Pallas kernels  68.9 us (99%)
  local copies, waits for them, and re-layouts  0.8 us (1%)
    pallas_call x1, Pallas kernels, body(): pl.pallas_call(functools.partial(tick_kernel, n_pipe, n_y), out_shape=plt...  68.9 us

profile of v2, /device:TPU:1, one launch (start us, length us, event | category | flops | bytes accessed | tf_op | source)
XLA Modules:
  0.0 69.7 jit_solution(11550746820132908699)
XLA Ops:
  0.0 68.9 %tick.1 = bf16[128,2048]{1,0:T(8,128)(2,1)S(1)} custom-call(s32[8,16]{1,0:T(8,128)} %bitcast.9, f32[1,2048]{1,0:T(1,128)} %gain_hbm.1, bf16[128,2048]{1,0:T(8,128)(2,1)} %bitcast.6, bf16[64,1536]{1,0:T(8,128)(2,1)} %bitcast.7, bf16[32,2048]{1,0:T(8,128)(2,1)} %bitcast.8), custom_call_target="tpu_custom_call" | custom-call | tf_op jit(solution)/shard_map/tick/pallas_call | solution.py:501
  68.9 0.8 %copy.7 = bf16[1,128,2048]{2,1,0:T(8,128)(2,1)} copy(bf16[1,128,2048]{2,1,0:T(8,128)(2,1)S(1)} %bitcast.5) | data formatting | bytes 1048576

commit v3 on v2

--- a/solution.py
+++ b/solution.py
@@ -16,7 +16,6 @@
 NX = 4
 CHUNKS = 2
 WINDOW = 9
-COLS = (GROUP + 2) * HEAD_DIM
 
 epsilon = 1e-05
 rope_base = 500000.0
@@ -64,7 +63,8 @@
     xn,
     wloc,
     wsp,
-    wi,
+    wkv,
+    wq,
     wo,
     trig,
     q_s,
@@ -130,7 +130,7 @@
     load_x = pltpu.make_async_copy(x_hbm, xg.at[0], local_sem.at[1])
     own_cols = pl.ds(pl.multiple_of(x * out_cols, out_cols), out_cols)
     load_o = pltpu.make_async_copy(
-        wo_hbm.at[:, own_cols], wo.at[y, x // 2, lax.rem(x, 2)], local_sem.at[2]
+        wo_hbm.at[:, own_cols], wo.at[y, x], local_sem.at[2]
     )
     load_g = pltpu.make_async_copy(gain_hbm, gain, local_sem.at[3])
     load_l = pltpu.make_async_copy(lengths_hbm, lengths, local_sem.at[4])
@@ -139,9 +139,8 @@
 
     barrier = pltpu.get_barrier_semaphore()
     peers = [(p, y, xs(d)) for d in (1, 2, 3)]
-    peers += [(p, ys(d), x) for d in (1, -1)]
-    peers += [(ps(e), y, xs(d)) for e in (1, -1) for d in range(NX)]
-    for peer in peers:
+    peers += [(p, ys(d), x) for d in (1, -1, -2)]
+    for peer in peers + [(ps(-1), y, xs(d)) for d in range(NX)]:
         pl.semaphore_signal(barrier, inc=1, device_id=peer, device_id_type=MESH)
     load_l.start()
     load_g.start()
@@ -162,62 +161,63 @@
             v_tile = pltpu.roll(v_tile, 64, 1)
         else:
             k_tile = pltpu.roll(k_tile, 64, 1)
-        wsp[t, :, :g_width] = wloc[:, g_width * t : g_width * (t + 1)]
-        wsp[t, :, g_width:] = jnp.where(lane_w < 64, k_tile, v_tile).astype(jnp.bfloat16)
-    wi[y, x] = wsp[x]
+        wsp[t] = jnp.where(lane_w < 64, k_tile, v_tile).astype(jnp.bfloat16)
+
+    def q_cols(d):
+        return pl.ds(pl.multiple_of(xs(d) * g_width, g_width), g_width)
+
+    wkv[y, x] = wsp[x]
+    wq[y, x] = wloc[:, q_cols(0)]
     load_x.wait()
     with jax.named_scope("barrier"):
-        pl.semaphore_wait(barrier, len(peers))
-
-    def place(buf, yy, xx):
-        return buf.at[yy, xx // 2, lax.rem(xx, 2)]
+        pl.semaphore_wait(barrier, len(peers) + NX)
 
     north, south = (p, ys(1), x), (p, ys(-1), x)
     toward = {1: north, -1: south}
     reach = n_y // 2
-
-    def piece_wi(dy, d):
-        return wi.at[ys(dy), xs(d)]
-
-    def piece_wo(dy, u):
-        return wo.at[ys(dy), u]
-
-    wi_order = ((0, 1), (0, -1), (-1, 1), (1, -1), (1, 1), (-1, -1), (2, 1), (2, -1))
-    wi_final = ((0, 1), (1, -1), (-1, 1), (2, -1))
-    wo_order = ((0, 1), (1, -1), (1, 1), (0, -1))
-    wo_final = ((0, 1), (1, -1))
-
-    def ring_send(piece, u, way, step):
-        source = piece(-way * step, u)
-        return send(source, source, toward[way], piece(-way * (step + 1), u))
-
-    def ring_step(piece, order, final, step, arrivals):
+    order = ((0, 1), (0, -1), (-1, 1), (-1, -1), (1, 1), (1, -1), (2, 1), (2, -1))
+    only_south = ((0, -1), (-1, -1), (1, -1), (2, -1))
+    shared = ((0, 1), (1, -1), (-1, 1), (2, -1))
+
+    def ring_send(buf, d, way, step):
+        source = buf.at[ys(-way * step), xs(d)]
+        return send(source, source, toward[way], buf.at[ys(-way * (step + 1)), xs(d)])
+
+    def ring_step(buf, final, step, arrivals):
         result = {}
         for key in order:
             if key not in arrivals:
                 continue
             arrivals[key]()
             if step + 1 < reach - 1 or (step + 1 == reach - 1 and key in final):
-                result[key] = ring_send(piece, key[0], key[1], step + 1)
+                result[key] = ring_send(buf, *key, step + 1)
         return result
 
-    wi_ring = {(0, way): ring_send(piece_wi, 0, way, 0) for way in (1, -1)}
-    wi_in = {
-        -d: send(wsp.at[xs(d)], piece_wi(0, 0), (p, y, xs(d)), piece_wi(0, -d))
-        for d in (1, -1)
-    }
-    wi_in[2] = send(wsp.at[xs(2)], piece_wi(0, 0), (p, y, xs(2)), piece_wi(0, 2))
+    def ring_own(buf):
+        return {(0, way): ring_send(buf, 0, way, 0) for way in (1, -1)}
+
+    def exchange(buf, source):
+        return {
+            -d % NX: send(source(d), buf.at[y, x], (p, y, xs(d)), buf.at[y, xs(-d)])
+            for d in (1, -1, 2)
+        }
+
+    def ring_join(buf, landed, ring):
+        for d in (-1, 1, 2):
+            landed[d % NX]()
+            for way in (1, -1):
+                ring[d, way] = ring_send(buf, d, way, 0)
+
+    kv_ring = ring_own(wkv)
+    kv_in = exchange(wkv, lambda d: wsp.at[xs(d)])
+    wq_ring = ring_own(wq)
+    wq_in = exchange(wq, lambda d: wloc.at[:, q_cols(d)])
     first, second = pl.ds(0, half), pl.ds(half, half)
     up, down = (p, y, xs(1)), (p, y, xs(-1))
     x_up_a = send(xg.at[0, first], xg.at[1, first], up)
     x_down_b = send(xg.at[0, second], xg.at[2, second], down)
     x_up_b = send(xg.at[0, second], xg.at[1, second], up)
     x_down_a = send(xg.at[0, first], xg.at[2, first], down)
-    for d in (-1, 1, 2):
-        with jax.named_scope(f"wi_in{d}"):
-            wi_in[d]()
-        for way in (1, -1):
-            wi_ring[d, way] = ring_send(piece_wi, d, way, 0)
 
     load_l.wait()
     load_g.wait()
@@ -260,45 +260,19 @@
             make_trig(slot)
     with jax.named_scope("norm0"):
         normalize(0)
-
-    with jax.named_scope("ring0"):
-        wi_ring = ring_step(piece_wi, wi_order, wi_final, 0, wi_ring)
-    with jax.named_scope("x_first"):
-        x_up_a()
-        x_far_a = send(xg.at[1, first], xg.at[3, first], up)
-        x_down_b()
-        x_far_b = send(xg.at[2, second], xg.at[3, second], down)
-    wo_in = []
-    for d in (1, -1, 2):
-        cols = pl.ds(pl.multiple_of(xs(d) * out_cols, out_cols), out_cols)
-        wo_in.append(
-            send(wo_hbm.at[:, cols], place(wo, y, x), (p, y, xs(d)), place(wo, y, xs(-d)))
-        )
-    with jax.named_scope("ring12"):
-        for step in range(1, reach - 1):
-            wi_ring = ring_step(piece_wi, wi_order, wi_final, step, wi_ring)
-    with jax.named_scope("x_second"):
-        x_up_b()
-        x_down_a()
-    with jax.named_scope("norm12"):
-        normalize(1)
-        normalize(2)
-    with jax.named_scope("ring3"):
-        wi_ring = ring_step(piece_wi, wi_order, wi_final, reach - 1, wi_ring)
-
     def rotated(tile, slot):
         partner = jnp.where((lane & 63) < 32, pltpu.roll(tile, 96, 1), pltpu.roll(tile, 32, 1))
         return tile * trig[slot, 0] + partner * trig[slot, 1]
 
-    def project(slot, count, first_col, last_col):
+    def project(slot, count, buf):
         return jnp.dot(
             xn[slot * rows : (slot + count) * rows, :],
-            wi[:, :, :, first_col:last_col].reshape(depth, last_col - first_col),
+            buf[...].reshape(depth, buf.shape[3]),
             preferred_element_type=jnp.float32,
         )
 
     def project_kv(slot, count):
-        proj = project(slot, count, g_width, COLS)
+        proj = project(slot, count, wkv)
         arrivals = []
         for i in range(count):
             own = proj[i * rows : (i + 1) * rows]
@@ -309,7 +283,7 @@
         return arrivals
 
     def project_q(slot, count):
-        proj = project(slot, count, 0, g_width)
+        proj = project(slot, count, wq)
         for i in range(count):
             own = proj[i * rows : (i + 1) * rows]
             block = xs(deltas[slot + i])
@@ -320,8 +294,55 @@
                     lane < 64, pltpu.roll(tile, 64, 1), 0.0
                 ).astype(jnp.bfloat16)
 
+    with jax.named_scope("kv_join"):
+        ring_join(wkv, kv_in, kv_ring)
+    with jax.named_scope("wq_join"):
+        ring_join(wq, wq_in, wq_ring)
+    with jax.named_scope("kv_ring0"):
+        kv_ring = ring_step(wkv, only_south, 0, kv_ring)
+    with jax.named_scope("wq_ring0"):
+        wq_ring = ring_step(wq, only_south, 0, wq_ring)
+    middle = range(1, reach - 1)
+    for step in middle[:1]:
+        with jax.named_scope("kv_ring1"):
+            kv_ring = ring_step(wkv, only_south, step, kv_ring)
+    with jax.named_scope("x_first"):
+        x_up_a()
+        x_far_a = send(xg.at[1, first], xg.at[3, first], up)
+        x_down_b()
+        x_far_b = send(xg.at[2, second], xg.at[3, second], down)
+
+    def o_cols(d):
+        return pl.ds(pl.multiple_of(xs(d) * out_cols, out_cols), out_cols)
+
+    wo_in = exchange(wo, lambda d: wo_hbm.at[:, o_cols(d)])
+    for step in middle[1:]:
+        with jax.named_scope("kv_ring2"):
+            kv_ring = ring_step(wkv, only_south, step, kv_ring)
+    for step in middle[:1]:
+        with jax.named_scope("wq_ring1"):
+            wq_ring = ring_step(wq, only_south, step, wq_ring)
+    with jax.named_scope("kv_ring3"):
+        ring_step(wkv, only_south, reach - 1, kv_ring)
+    with jax.named_scope("x_second"):
+        x_up_b()
+        x_down_a()
+    with jax.named_scope("norm12"):
+        normalize(1)
+        normalize(2)
     with jax.named_scope("kv012"):
         near = project_kv(0, 3)
+    for step in middle[1:]:
+        with jax.named_scope("wq_ring2"):
+            wq_ring = ring_step(wq, only_south, step, wq_ring)
+    load_o.wait()
+    wo_ring = ring_own(wo)
+    far = []
+    with jax.named_scope("kv_near"):
+        for slot in range(3):
+            near[slot]()
+            block = xs(deltas[slot])
+            far.append(send(kv.at[NX + block], kv.at[block], north))
     with jax.named_scope("x_far"):
         x_far_a()
         x_far_b()
@@ -330,20 +351,13 @@
     with jax.named_scope("kv3"):
         near += project_kv(3, 1)
     block = xs(deltas[3])
-    far = [send(kv.at[2 * NX + block], kv.at[block], (p, ys(2), x))]
-    with jax.named_scope("wo_in"):
-        load_o.wait()
-        for arrive in wo_in:
-            arrive()
-    wo_ring = {key: ring_send(piece_wo, *key, 0) for key in wo_order if key[1] == -1}
+    far.append(send(kv.at[2 * NX + block], kv.at[block], (p, ys(2), x)))
+    with jax.named_scope("wq_ring3"):
+        ring_step(wq, only_south, reach - 1, wq_ring)
     with jax.named_scope("q012"):
         project_q(0, 3)
-    with jax.named_scope("kv_near"):
-        for slot in range(3):
-            near[slot]()
-            block = xs(deltas[slot])
-            far.append(send(kv.at[NX + block], kv.at[block], north))
-    wo_ring.update({key: ring_send(piece_wo, *key, 0) for key in wo_order if key[1] == 1})
+    with jax.named_scope("wo_join"):
+        ring_join(wo, wo_in, wo_ring)
     with jax.named_scope("q3"):
         project_q(3, 1)
     with jax.named_scope("kv_far"):
@@ -446,7 +460,7 @@
         attend(0, 0)
         attend(0, 1)
     with jax.named_scope("wo0"):
-        wo_ring = ring_step(piece_wo, wo_order, wo_final, 0, wo_ring)
+        wo_ring = ring_step(wo, shared, 0, wo_ring)
     with jax.named_scope("attend0b"):
         attend(0, 2)
         attend(0, 3)
@@ -456,7 +470,7 @@
         attend(1, 1)
     for step in range(1, reach - 2):
         with jax.named_scope("wo1"):
-            wo_ring = ring_step(piece_wo, wo_order, wo_final, step, wo_ring)
+            wo_ring = ring_step(wo, shared, step, wo_ring)
     with jax.named_scope("attend1b"):
         attend(1, 2)
         attend(1, 3)
@@ -465,14 +479,14 @@
     arrivals_1 = att_start(1)
     with jax.named_scope("wo2"):
         if reach > 2:
-            wo_ring = ring_step(piece_wo, wo_order, wo_final, reach - 2, wo_ring)
+            wo_ring = ring_step(wo, shared, reach - 2, wo_ring)
     with jax.named_scope("att0_in"):
         for arrive in arrivals_0:
             arrive()
     with jax.named_scope("pass1"):
         arrivals_1 = att_pass(1, arrivals_1)
     with jax.named_scope("wo3"):
-        wo_ring = ring_step(piece_wo, wo_order, wo_final, reach - 1, wo_ring)
+        wo_ring = ring_step(wo, shared, reach - 1, wo_ring)
     with jax.named_scope("finish0"):
         last = finish(0)
     with jax.named_scope("att1_in"):
@@ -496,7 +510,7 @@
     n_pipe = lax.axis_size("pipe")
     n_y = lax.axis_size("ctx_y")
     part = rows // CHUNKS
-    copies = 128
+    copies = 160
     bf16, f32 = jnp.bfloat16, jnp.float32
     moved = pl.pallas_call(
         functools.partial(tick_kernel, n_pipe, n_y),
@@ -515,9 +529,10 @@
             pltpu.VMEM((4, rows, depth), bf16),
             pltpu.VMEM((4 * rows, depth), bf16),
             pltpu.VMEM((w_rows, w_in.shape[2]), bf16),
-            pltpu.VMEM((NX, w_rows, COLS), bf16),
-            pltpu.VMEM((n_y, NX, w_rows, COLS), bf16),
-            pltpu.VMEM((n_y, 2, 2, o_rows, out_cols), bf16),
+            pltpu.VMEM((NX, w_rows, 128), bf16),
+            pltpu.VMEM((n_y, NX, w_rows, 128), bf16),
+            pltpu.VMEM((n_y, NX, w_rows, GROUP * HEAD_DIM), bf16),
+            pltpu.VMEM((n_y, NX, o_rows, out_cols), bf16),
             pltpu.VMEM((4, 2, rows, 128), f32),
             pltpu.VMEM((NX, GROUP, rows, 128), bf16),
             pltpu.VMEM((3 * NX, rows, 128), bf16),

time: 69.8 us -> 64 us (0.917); the launches traced: 69.7 us -> 62.9 us
  Pallas kernels: 68.9 us -> 62.1 us
    pallas_call x1, Pallas kernels: 68.9 us -> 62.1 us  [body(): pl.pallas_call(functools.partial(tick_kernel, n_pipe, n_y), out_shape=plt...]
where the time goes in v3:
time: 64 us; the launch traced here: 62.9 us
  Pallas kernels  62.1 us (97%)
  local copies, waits for them, and re-layouts  0.8 us (1%)
    pallas_call x1, Pallas kernels, body(): pl.pallas_call(functools.partial(tick_kernel, n_pipe, n_y), out_shape=plt...  62.1 us

profile of v3, /device:TPU:1, one launch (start us, length us, event | category | flops | bytes accessed | tf_op | source)
XLA Modules:
  0.0 62.9 jit_solution(15905283320077929911)
XLA Ops:
  0.0 62.1 %tick.1 = bf16[128,2048]{1,0:T(8,128)(2,1)S(1)} custom-call(s32[8,16]{1,0:T(8,128)} %bitcast.9, f32[1,2048]{1,0:T(1,128)} %gain_hbm.1, bf16[128,2048]{1,0:T(8,128)(2,1)} %bitcast.6, bf16[64,1536]{1,0:T(8,128)(2,1)} %bitcast.7, bf16[32,2048]{1,0:T(8,128)(2,1)} %bitcast.8), custom_call_target="tpu_custom_call" | custom-call | tf_op jit(solution)/shard_map/tick/pallas_call | solution.py:515
  62.1 0.8 %copy.7 = bf16[1,128,2048]{2,1,0:T(8,128)(2,1)} copy(bf16[1,128,2048]{2,1,0:T(8,128)(2,1)S(1)} %bitcast.5) | data formatting | bytes 1048576

commit v4 on v3

v4 whole, which is shorter than its diff:
```python
import functools
import math

import jax
import jax.numpy as jnp
from jax import lax
from jax.experimental import pallas as pl
from jax.experimental.pallas import tpu as pltpu
from jax.sharding import Mesh
from jax.sharding import PartitionSpec as P

HEAD_DIM = 64
HEADS = 16
KV_HEADS = 4
GROUP = HEADS // KV_HEADS
NX = 4
CHUNKS = 2
WINDOW = 9

epsilon = 1e-05
rope_base = 500000.0
masked_score = -1e30
MESH = pl.DeviceIdType.MESH


def sine_cosine(angle):
    turns = jnp.floor(angle * (2.0 / math.pi) + 0.5)
    quarter = turns.astype(jnp.int32)
    rest = angle - turns * 1.5703125
    rest = rest - turns * 4.837512969970703125e-4
    rest = rest - turns * 7.54978995489188216e-8
    z = rest * rest
    sine = ((-1.9515295891e-4 * z + 8.3321608736e-3) * z - 1.6666654611e-1) * z * rest + rest
    cosine = (
        (2.443315711809948e-5 * z - 1.388731625493765e-3) * z + 4.166664568298827e-2
    ) * z * z - 0.5 * z + 1.0
    odd = (quarter & 1) == 1
    sine, cosine = jnp.where(odd, cosine, sine), jnp.where(odd, sine, cosine)
    sine = jnp.where((quarter & 2) == 2, -sine, sine)
    cosine = jnp.where(((quarter + 1) & 2) == 2, -cosine, cosine)
    return sine, cosine


def response_start(ends, spots):
    start = jnp.zeros_like(spots)
    for end in ends:
        start = jnp.maximum(start, jnp.where(spots >= end, end, 0))
    return start


def tick_kernel(
    n_pipe,
    n_y,
    lengths_hbm,
    gain_hbm,
    x_hbm,
    wi_hbm,
    wo_hbm,
    out,
    lengths,
    gain,
    xg,
    xn,
    wloc,
    wsp,
    wkv,
    wq,
    wo,
    trig,
    masks,
    q_s,
    kv,
    v_one,
    att,
    acc,
    obuf,
    local_sem,
    send_sem,
    recv_sem,
):
    p = lax.axis_index("pipe")
    y = lax.axis_index("ctx_y")
    x = lax.axis_index("ctx_x")
    rows = xg.shape[1]
    half = rows // 2
    part = rows // CHUNKS
    depth = xg.shape[2]
    out_cols = acc.shape[1]
    span = NX * rows

    def xs(d):
        return lax.rem(x + (d + NX), NX)

    def ys(d):
        return lax.rem(y + (d + n_y), n_y)

    def ps(d):
        return lax.rem(p + (d + n_pipe), n_pipe)

    slots = {}
    sources = {}

    def copy_of(name, src, dst, device):
        k = slots.setdefault(name, len(slots))
        return pltpu.make_async_remote_copy(
            src_ref=src,
            dst_ref=dst,
            send_sem=send_sem.at[k],
            recv_sem=recv_sem.at[k],
            device_id=device,
            device_id_type=MESH,
        )

    def send(name, src, device, dst=None):
        sources[name] = src
        copy_of(name, src(), src() if dst is None else dst(), device).start()

    def land(name, dst):
        copy_of(name, dst, dst, (p, y, x)).wait_recv()

    load_w = pltpu.make_async_copy(wi_hbm, wloc, local_sem.at[0])
    load_x = pltpu.make_async_copy(x_hbm, xg.at[0], local_sem.at[1])
    own_cols = pl.ds(pl.multiple_of(x * out_cols, out_cols), out_cols)
    load_o = pltpu.make_async_copy(
        wo_hbm.at[:, own_cols], wo.at[y, x], local_sem.at[2]
    )
    load_g = pltpu.make_async_copy(gain_hbm, gain, local_sem.at[3])
    load_l = pltpu.make_async_copy(lengths_hbm, lengths, local_sem.at[4])
    load_w.start()
    load_x.start()

    barrier = pltpu.get_barrier_semaphore()
    peers = [(p, y, xs(d)) for d in (1, 2, 3)]
    peers += [(p, ys(d), x) for d in (1, -1)]
    peers += [(p, ys(-2), x)]
    for peer in peers + [(ps(-1), y, xs(d)) for d in range(NX)]:
        pl.semaphore_signal(barrier, inc=1, device_id=peer, device_id_type=MESH)
    load_l.start()
    load_g.start()
    load_o.start()

    load_w.wait()
    w_rows = wloc.shape[0]
    lane_w = lax.broadcasted_iota(jnp.int32, (w_rows, 128), 1)
    q_width = HEADS * HEAD_DIM
    g_width = GROUP * HEAD_DIM
    for t in range(NX):
        k_tile = wloc[:, q_width + 128 * (t // 2) : q_width + 128 * (t // 2) + 128]
        v_at = q_width + KV_HEADS * HEAD_DIM + 128 * (t // 2)
        v_tile = wloc[:, v_at : v_at + 128]
        k_tile = k_tile.astype(jnp.float32)
        v_tile = v_tile.astype(jnp.float32)
        if t % 2 == 0:
            v_tile = pltpu.roll(v_tile, 64, 1)
        else:
            k_tile = pltpu.roll(k_tile, 64, 1)
        wsp[t] = jnp.where(lane_w < 64, k_tile, v_tile).astype(jnp.bfloat16)

    def q_cols(d):
        return pl.ds(pl.multiple_of(xs(d) * g_width, g_width), g_width)

    wkv[y, x] = wsp[x]
    wq[y, x] = wloc[:, q_cols(0)]
    load_x.wait()
    with jax.named_scope("barrier"):
        pl.semaphore_wait(barrier, len(peers) + NX)

    north, south = (p, ys(1), x), (p, ys(-1), x)
    up, down = (p, y, xs(1)), (p, y, xs(-1))
    toward = {1: north, -1: south}
    reach = n_y // 2
    order = ((0, 1), (0, -1), (-1, 1), (-1, -1), (1, 1), (1, -1), (2, 1), (2, -1))
    only_south = ((0, -1), (-1, -1), (1, -1), (2, -1))
    rings = {"kv": (wkv, only_south), "q": (wq, only_south), "o": (wo, only_south)}

    def ring_send(ring, d, way, step):
        buf = rings[ring][0]
        send(
            (ring, d, way, step),
            lambda: buf.at[ys(-way * step), xs(d)],
            toward[way],
        )

    def ring_step(ring, step, pieces=order):
        buf, final = rings[ring]
        if not 0 <= step < reach:
            return
        with jax.named_scope(f"{ring}_ring{step}"):
            for d, way in pieces:
                if step == reach - 1 and (d, way) not in final:
                    continue
                land((ring, d, way, step), buf.at[ys(-way * (step + 1)), xs(d)])
                if step + 1 < reach - 1 or (step + 1 == reach - 1 and (d, way) in final):
                    ring_send(ring, d, way, step + 1)

    def ring_steps(ring, *steps):
        for step in steps:
            if 0 <= step < reach - 1:
                ring_step(ring, step)

    def ring_own(ring):
        for way in (1, -1):
            ring_send(ring, 0, way, 0)

    def exchange(ring, source):
        buf = rings[ring][0]
        for d in (1, -1, 2):
            send((ring, d), lambda d=d: source(d), (p, y, xs(d)), lambda: buf.at[y, x])

    def ring_join(ring, *ways):
        with jax.named_scope(f"{ring}_join"):
            for d in (1, -1, 2):
                land((ring, d), rings[ring][0].at[y, xs(-d)])
                e = d if d == 2 else -d
                for way in ways:
                    ring_send(ring, e, way, 0)

    first, second = pl.ds(0, half), pl.ds(half, half)

    def x_start():
        send("x_up_a", lambda: xg.at[0, first], up, lambda: xg.at[1, first])
        send("x_down_b", lambda: xg.at[0, second], down, lambda: xg.at[2, second])
        send("x_up_b", lambda: xg.at[0, second], up, lambda: xg.at[1, second])
        send("x_down_a", lambda: xg.at[0, first], down, lambda: xg.at[2, first])

    def x_pass():
        with jax.named_scope("x_first"):
            land("x_up_a", xg.at[1, first])
            send("x_far_a", lambda: xg.at[1, first], up, lambda: xg.at[3, first])
            land("x_down_b", xg.at[2, second])
            send("x_far_b", lambda: xg.at[2, second], down, lambda: xg.at[3, second])

    def x_second():
        with jax.named_scope("x_second"):
            land("x_up_b", xg.at[1, second])
            land("x_down_a", xg.at[2, first])

    def x_far():
        with jax.named_scope("x_far"):
            land("x_far_a", xg.at[3, first])
            land("x_far_b", xg.at[3, second])

    def kv_exchange():
        exchange("kv", lambda d: wsp.at[xs(d)])

    def q_exchange():
        exchange("q", lambda d: wloc.at[:, q_cols(d)])

    def o_exchange():
        exchange("o", lambda d: wo_hbm.at[:, o_cols(d)])

    def o_cols(d):
        return pl.ds(pl.multiple_of(xs(d) * out_cols, out_cols), out_cols)

    load_l.wait()
    load_g.wait()
    ends = []
    total = 0
    for i in range(lengths.shape[0]):
        total = total + lengths[i, p]
        ends.append(total)
    deltas = (0, -1, 1, 2)
    lane = lax.broadcasted_iota(jnp.int32, (rows, 128), 1)
    row = lax.broadcasted_iota(jnp.int32, (rows, 128), 0)
    half_dim = HEAD_DIM // 2
    turn = lax.broadcasted_iota(jnp.int32, (8, 128), 1) & (half_dim - 1)
    inverse = jnp.zeros((8, 128), jnp.float32)
    for i in range(half_dim):
        inverse = jnp.where(turn == i, rope_base ** (-2.0 * i / HEAD_DIM), inverse)

    def make_trig(slot):
        spots = y * span + xs(deltas[slot]) * rows + row
        place_in = (spots - response_start(ends, spots)).astype(jnp.float32)
        sine, cosine = sine_cosine(place_in * inverse[:1])
        trig[slot, 0] = cosine
        trig[slot, 1] = jnp.where((lane & 63) < 32, -sine, sine)

    norm_rows = 32

    def normalize(slot):
        def step(i, carry):
            at = pl.ds(pl.multiple_of(i * norm_rows, norm_rows), norm_rows)
            wide = xg[slot, at, :].astype(jnp.float32)
            scale = lax.rsqrt(jnp.mean(wide * wide, -1, keepdims=True) + epsilon)
            to = pl.ds(pl.multiple_of(slot * rows + i * norm_rows, norm_rows), norm_rows)
            xn[to, :] = (wide * scale * gain[...]).astype(jnp.bfloat16)
            return carry

        lax.fori_loop(0, rows // norm_rows, step, 0, unroll=2)

    def rotated(tile, slot):
        partner = jnp.where((lane & 63) < 32, pltpu.roll(tile, 96, 1), pltpu.roll(tile, 32, 1))
        return tile * trig[slot, 0] + partner * trig[slot, 1]

    def project(slot, count, buf):
        return jnp.dot(
            xn[slot * rows : (slot + count) * rows, :],
            buf[...].reshape(depth, buf.shape[3]),
            preferred_element_type=jnp.float32,
        )

    def own_kv(slot):
        return kv.at[2 * NX + xs(deltas[slot])]

    def near_kv(slot):
        return kv.at[NX + xs(deltas[slot])]

    def far_kv(slot):
        return kv.at[xs(deltas[slot])]

    def project_kv(slot, count):
        with jax.named_scope(f"kv{slot}"):
            proj = project(slot, count, wkv)
            for i in range(count):
                own = proj[i * rows : (i + 1) * rows]
                own = jnp.where(lane < 64, rotated(own, slot + i), own)
                kv[2 * NX + xs(deltas[slot + i])] = own.astype(jnp.bfloat16)
                send(
                    ("far", slot + i),
                    lambda i=i: own_kv(slot + i),
                    (p, ys(2), x),
                    lambda i=i: far_kv(slot + i),
                )
                send(
                    ("near", slot + i),
                    lambda i=i: own_kv(slot + i),
                    north,
                    lambda i=i: near_kv(slot + i),
                )

    def project_q(slot, count):
        proj = project(slot, count, wq)
        for i in range(count):
            own = proj[i * rows : (i + 1) * rows]
            block = xs(deltas[slot + i])
            for t in range(GROUP // 2):
                tile = rotated(own[:, 128 * t : 128 * (t + 1)], slot + i) * HEAD_DIM**-0.5
                q_s[block, 2 * t] = jnp.where(lane < 64, tile, 0.0).astype(jnp.bfloat16)
                q_s[block, 2 * t + 1] = jnp.where(
                    lane < 64, pltpu.roll(tile, 64, 1), 0.0
                ).astype(jnp.bfloat16)

    lane_p = lax.broadcasted_iota(jnp.int32, (part, 128), 1)
    row_p = lax.broadcasted_iota(jnp.int32, (part, 128), 0)

    def make_masks(i):
        def one(j, carry):
            spots = y * span + j * rows + i * part + row_p
            start = response_start(ends, spots)
            for c in range(WINDOW):
                keys = y * span + (j + c - 2 * NX) * rows + lane_p
                inside = keys >= start
                if c == WINDOW - 1:
                    inside = inside & (keys <= spots)
                masks[i, j, :, c * rows : (c + 1) * rows] = jnp.where(inside, 0.0, masked_score)
            return carry

        lax.fori_loop(0, NX, one, 0)

    def prepare():
        with jax.named_scope("trig"):
            for slot in range(4):
                make_trig(slot)
        with jax.named_scope("norm0"):
            normalize(0)
        with jax.named_scope("masks"):
            for i in range(CHUNKS):
                make_masks(i)

    def norms(*which):
        with jax.named_scope("norms"):
            for slot in which:
                normalize(slot)

    def last_block():
        x_far()
        norms(3)
        project_kv(3, 1)

    def queries_of(slot, count):
        with jax.named_scope(f"q{slot}"):
            project_q(slot, count)

    late = lax.rem(p + p // (n_pipe - 2), 2) == 1
    ring_own("kv")
    kv_exchange()
    ring_own("q")
    q_exchange()

    @pl.when(jnp.logical_not(late))
    def _():
        x_start()

    prepare()
    ring_join("kv", 1, -1)

    @pl.when(late)
    def _():
        x_start()

    ring_join("q", 1, -1)
    ring_steps("kv", 0)
    ring_steps("q", 0)
    ring_steps("kv", 1)
    x_pass()
    o_exchange()
    ring_steps("kv", *range(2, reach))
    ring_steps("q", 1)
    ring_step("kv", reach - 1)
    x_second()
    norms(1, 2)
    project_kv(0, 3)
    ring_steps("q", *range(2, reach))
    last_block()
    going_north = ((-1, 1), (1, 1), (2, 1))
    going_south = ((-1, -1), (1, -1), (2, -1))
    load_o.wait()
    ring_send("o", 0, -1, 0)
    ring_join("o", -1)
    ring_step("q", reach - 1)
    queries_of(0, 3)
    queries_of(3, 1)
    with jax.named_scope("kv_near"):
        for slot in range(4):
            land(("near", slot), near_kv(slot))
    for d in (0, -1, 1, 2):
        ring_send("o", d, 1, 0)
    ring_step("o", 0, ((0, -1),) + going_south)
    with jax.named_scope("kv_far"):
        for slot in range(4):
            land(("far", slot), far_kv(slot))
    with jax.named_scope("v_one"):
        for b in range(3 * NX):
            v_one[b] = jnp.where(lane < 64, 1.0, kv[b].astype(jnp.float32)).astype(jnp.bfloat16)

    def attend(i, j):
        queries = q_s[j, :, i * part : (i + 1) * part, :].reshape(GROUP * part, 128)
        window = kv[j : j + WINDOW].reshape(WINDOW * rows, 128)
        values = v_one[j : j + WINDOW].reshape(WINDOW * rows, 128)
        scores = lax.dot_general(
            queries, window, (((1,), (1,)), ((), ())), preferred_element_type=jnp.float32
        )
        scores = scores.reshape(GROUP, part, WINDOW * rows) + masks[i, j][None]
        probs = jnp.exp(scores - jnp.max(scores, -1, keepdims=True))
        mixed = jnp.dot(
            probs.astype(jnp.bfloat16).reshape(GROUP * part, WINDOW * rows),
            values,
            preferred_element_type=jnp.float32,
        )
        turned = pltpu.roll(mixed, 64, 1)
        tiles = []
        for t in range(GROUP // 2):
            even = slice(2 * t * part, (2 * t + 1) * part)
            odd = slice((2 * t + 1) * part, (2 * t + 2) * part)
            tiles.append(
                jnp.where(lane_p < 64, turned[even] / mixed[even], mixed[odd] / turned[odd])
            )
        att[i, x, j] = jnp.concatenate(tiles, 1).astype(jnp.bfloat16)

    low, high = pl.ds(0, NX // 2), pl.ds(NX // 2, NX // 2)

    def piece(i, d, which):
        return att.at[i, xs(d), which]

    def att_start(i):
        send(("up_l", i), lambda: piece(i, 0, low), up)
        send(("down_h", i), lambda: piece(i, 0, high), down)
        send(("up_h", i), lambda: piece(i, 0, high), up)
        send(("down_l", i), lambda: piece(i, 0, low), down)

    def att_pass(i):
        with jax.named_scope(f"pass{i}"):
            land(("up_l", i), piece(i, -1, low))
            send(("far_l", i), lambda: piece(i, -1, low), up)
            land(("down_h", i), piece(i, 1, high))
            send(("far_h", i), lambda: piece(i, 1, high), down)

    def att_in(i):
        with jax.named_scope(f"att{i}_in"):
            land(("up_h", i), piece(i, -1, high))
            land(("down_l", i), piece(i, 1, low))
            land(("far_l", i), piece(i, 2, low))
            land(("far_h", i), piece(i, 2, high))

    def out_part(i, d):
        return out.at[pl.ds(i * part, part), o_cols(d)]

    def finish(i):
        weight = wo[...].reshape(q_width, out_cols)
        result = None
        for h in range(NX):
            term = jnp.dot(
                att[i, h].reshape(NX * part, g_width),
                weight[h * g_width : (h + 1) * g_width],
                preferred_element_type=jnp.float32,
            )
            result = term if result is None else result + term
        acc[...] = result
        for slot in (3, 2, 1, 0):
            j = xs(deltas[slot])
            kept = xg[slot, i * part : (i + 1) * part, own_cols].astype(jnp.float32)
            at = pl.ds(pl.multiple_of(j * part, part), part)
            obuf[i, slot] = (acc[at, :] + kept).astype(jnp.bfloat16)
            send(
                ("out", i, slot),
                lambda slot=slot: obuf.at[i, slot],
                (ps(1), y, j),
                lambda: out_part(i, 0),
            )

    def o_steps(step, pieces):
        if step < reach - 1:
            ring_step("o", step, pieces)

    with jax.named_scope("attend0a"):
        attend(0, 0)
        attend(0, 1)
    with jax.named_scope("attend0b"):
        attend(0, 2)
        attend(0, 3)
    att_start(0)
    with jax.named_scope("attend1a"):
        attend(1, 0)
        attend(1, 1)
    ring_step("o", 0, ((0, 1),) + going_north)
    o_steps(1, ((0, -1),) + going_south)
    with jax.named_scope("attend1b"):
        attend(1, 2)
        attend(1, 3)
    att_pass(0)
    att_start(1)
    o_steps(1, ((0, 1),) + going_north)
    for step in range(2, reach - 1):
        o_steps(step, ((0, -1),) + going_south)
    att_in(0)
    att_pass(1)
    for step in range(2, reach - 1):
        o_steps(step, ((0, 1),) + going_north)
    ring_step("o", reach - 1)
    with jax.named_scope("finish0"):
        finish(0)
    att_in(1)
    with jax.named_scope("finish1"):
        finish(1)
    with jax.named_scope("out_in"):
        for i in range(CHUNKS):
            for slot in (3, 2, 1, 0):
                land(("out", i, slot), out_part(i, -deltas[slot]))
    with jax.named_scope("wait_send"):
        for name, src in sources.items():
            copy_of(name, src(), src(), (p, y, x)).wait_send()


def body(states, norm_gain, w_in, w_out, lengths):
    rows, depth = states.shape[1:]
    w_rows = w_in.shape[1]
    o_rows = w_out.shape[1]
    out_cols = depth // NX
    n_pipe = lax.axis_size("pipe")
    n_y = lax.axis_size("ctx_y")
    part = rows // CHUNKS
    copies = 160
    bf16, f32 = jnp.bfloat16, jnp.float32
    moved = pl.pallas_call(
        functools.partial(tick_kernel, n_pipe, n_y),
        out_shape=pltpu.VMEM((rows, depth), bf16),
        in_specs=[
            pl.BlockSpec(memory_space=pl.ANY),
            pl.BlockSpec(memory_space=pl.ANY),
            pl.BlockSpec(memory_space=pl.ANY),
            pl.BlockSpec(memory_space=pl.ANY),
            pl.BlockSpec(memory_space=pl.ANY),
        ],
        out_specs=pl.BlockSpec(memory_space=pltpu.VMEM),
        scratch_shapes=[
            pltpu.SMEM(lengths.shape[::-1], jnp.int32),
            pltpu.VMEM((1, depth), f32),
            pltpu.VMEM((4, rows, depth), bf16),
            pltpu.VMEM((4 * rows, depth), bf16),
            pltpu.VMEM((w_rows, w_in.shape[2]), bf16),
            pltpu.VMEM((NX, w_rows, 128), bf16),
            pltpu.VMEM((n_y, NX, w_rows, 128), bf16),
            pltpu.VMEM((n_y, NX, w_rows, GROUP * HEAD_DIM), bf16),
            pltpu.VMEM((n_y, NX, o_rows, out_cols), bf16),
            pltpu.VMEM((4, 2, rows, 128), f32),
            pltpu.VMEM((CHUNKS, NX, part, WINDOW * rows), f32),
            pltpu.VMEM((NX, GROUP, rows, 128), bf16),
            pltpu.VMEM((3 * NX, rows, 128), bf16),
            pltpu.VMEM((3 * NX, rows, 128), bf16),
            pltpu.VMEM((CHUNKS, NX, NX, part, GROUP * HEAD_DIM), bf16),
            pltpu.VMEM((NX * part, out_cols), f32),
            pltpu.VMEM((CHUNKS, 4, part, out_cols), bf16),
            pltpu.SemaphoreType.DMA((5,)),
            pltpu.SemaphoreType.DMA((copies,)),
            pltpu.SemaphoreType.DMA((copies,)),
        ],
        compiler_params=pltpu.CompilerParams(
            collective_id=0, has_side_effects=True, vmem_limit_bytes=60 * 1024 * 1024
        ),
        name="tick",
    )(lengths.T, norm_gain, states[0], w_in[0], w_out[0])
    return moved[None]


def solution(mesh):
    n_pipe = mesh.shape["pipe"]
    n_y = mesh.shape["ctx"] // NX
    finer = Mesh(mesh.devices.reshape(n_pipe, n_y, NX), ("pipe", "ctx_y", "ctx_x"))
    ctx = ("ctx_y", "ctx_x")
    placed = (
        P("pipe", ctx, None),
        P("pipe", None),
        P("pipe", ctx, None),
        P("pipe", ctx, None),
        P(),
    )
    return jax.shard_map(
        body, mesh=finer, in_specs=placed, out_specs=P("pipe", ctx, None), check_vma=False
    )
```

time: 64 us -> 63.5 us (level)
  no operation moved by 1% of the time
where the time goes in v4:
time: 63.5 us; the launch traced here: 62.7 us
  Pallas kernels  61.9 us (97%)
  local copies, waits for them, and re-layouts  0.8 us (1%)
    pallas_call x1, Pallas kernels, body(): pl.pallas_call(functools.partial(tick_kernel, n_pipe, n_y), out_shape=plt...  61.9 us

profile of v4, /device:TPU:1, one launch (start us, length us, event | category | flops | bytes accessed | tf_op | source)
XLA Modules:
  0.0 62.7 jit_solution(15519343599996931527)
XLA Ops:
  0.0 61.9 %tick.1 = bf16[128,2048]{1,0:T(8,128)(2,1)S(1)} custom-call(s32[8,16]{1,0:T(8,128)} %bitcast.9, f32[1,2048]{1,0:T(1,128)} %gain_hbm.1, bf16[128,2048]{1,0:T(8,128)(2,1)} %bitcast.6, bf16[64,1536]{1,0:T(8,128)(2,1)} %bitcast.7, bf16[32,2048]{1,0:T(8,128)(2,1)} %bitcast.8), custom_call_target="tpu_custom_call" | custom-call | tf_op jit(solution)/shard_map/tick/pallas_call | solution.py:564
  61.9 0.8 %copy.7 = bf16[1,128,2048]{2,1,0:T(8,128)(2,1)} copy(bf16[1,128,2048]{2,1,0:T(8,128)(2,1)S(1)} %bitcast.5) | data formatting | bytes 1048576

commit v5 on v4

--- a/solution.py
+++ b/solution.py
@@ -315,18 +315,25 @@
                 own = proj[i * rows : (i + 1) * rows]
                 own = jnp.where(lane < 64, rotated(own, slot + i), own)
                 kv[2 * NX + xs(deltas[slot + i])] = own.astype(jnp.bfloat16)
-                send(
-                    ("far", slot + i),
-                    lambda i=i: own_kv(slot + i),
-                    (p, ys(2), x),
-                    lambda i=i: far_kv(slot + i),
-                )
+                if slot + i == 3:
+                    send(
+                        ("far", 3),
+                        lambda: own_kv(3),
+                        (p, ys(2), x),
+                        lambda: far_kv(3),
+                    )
                 send(
                     ("near", slot + i),
                     lambda i=i: own_kv(slot + i),
                     north,
                     lambda i=i: near_kv(slot + i),
                 )
+
+    def kv_pass():
+        with jax.named_scope("kv_pass"):
+            for slot in range(3):
+                land(("near", slot), near_kv(slot))
+                send(("far", slot), lambda slot=slot: near_kv(slot), north, lambda: far_kv(slot))
 
     def project_q(slot, count):
         proj = project(slot, count, wq)
@@ -394,11 +401,18 @@
     prepare()
     ring_join("kv", 1, -1)
 
-    @pl.when(late)
+    later = jnp.logical_or(p == n_pipe - 2, p == 1)
+
+    @pl.when(jnp.logical_and(late, jnp.logical_not(later)))
     def _():
         x_start()
 
     ring_join("q", 1, -1)
+
+    @pl.when(later)
+    def _():
+        x_start()
+
     ring_steps("kv", 0)
     ring_steps("q", 0)
     ring_steps("kv", 1)
@@ -415,17 +429,16 @@
     going_north = ((-1, 1), (1, 1), (2, 1))
     going_south = ((-1, -1), (1, -1), (2, -1))
     load_o.wait()
+    kv_pass()
     ring_send("o", 0, -1, 0)
     ring_join("o", -1)
     ring_step("q", reach - 1)
     queries_of(0, 3)
     queries_of(3, 1)
     with jax.named_scope("kv_near"):
-        for slot in range(4):
-            land(("near", slot), near_kv(slot))
+        land(("near", 3), near_kv(3))
     for d in (0, -1, 1, 2):
         ring_send("o", d, 1, 0)
-    ring_step("o", 0, ((0, -1),) + going_south)
     with jax.named_scope("kv_far"):
         for slot in range(4):
             land(("far", slot), far_kv(slot))
@@ -512,9 +525,9 @@
         if step < reach - 1:
             ring_step("o", step, pieces)
 
-    with jax.named_scope("attend0a"):
-        attend(0, 0)
-        attend(0, 1)
+    attend(0, 0)
+    ring_step("o", 0, ((0, -1),) + going_south)
+    attend(0, 1)
     with jax.named_scope("attend0b"):
         attend(0, 2)
         attend(0, 3)

time: 63.5 us -> 62.9 us (level); the launches traced: 62.7 us -> 62.8 us
  no operation moved by 1% of the time
where the time goes in v5:
time: 62.9 us; the launch traced here: 62.8 us
  Pallas kernels  62 us (99%)
  local copies, waits for them, and re-layouts  0.8 us (1%)
    pallas_call x1, Pallas kernels, body(): pl.pallas_call(functools.partial(tick_kernel, n_pipe, n_y), out_shape=plt...  62 us

profile of v5, /device:TPU:1, one launch (start us, length us, event | category | flops | bytes accessed | tf_op | source)
XLA Modules:
  0.0 62.8 jit_solution(14046532839917583243)
XLA Ops:
  0.0 62.0 %tick.1 = bf16[128,2048]{1,0:T(8,128)(2,1)S(1)} custom-call(s32[8,16]{1,0:T(8,128)} %bitcast.9, f32[1,2048]{1,0:T(1,128)} %gain_hbm.1, bf16[128,2048]{1,0:T(8,128)(2,1)} %bitcast.6, bf16[64,1536]{1,0:T(8,128)(2,1)} %bitcast.7, bf16[32,2048]{1,0:T(8,128)(2,1)} %bitcast.8), custom_call_target="tpu_custom_call" | custom-call | tf_op jit(solution)/shard_map/tick/pallas_call | solution.py:577
  62.0 0.8 %copy.7 = bf16[1,128,2048]{2,1,0:T(8,128)(2,1)} copy(bf16[1,128,2048]{2,1,0:T(8,128)(2,1)S(1)} %bitcast.5) | data formatting | bytes 1048576

commit v6 on v5

--- a/solution.py
+++ b/solution.py
@@ -475,6 +475,14 @@
     def piece(i, d, which):
         return att.at[i, xs(d), which]
 
+    def att_low(i):
+        send(("up_l", i), lambda: piece(i, 0, low), up)
+        send(("down_l", i), lambda: piece(i, 0, low), down)
+
+    def att_high(i):
+        send(("down_h", i), lambda: piece(i, 0, high), down)
+        send(("up_h", i), lambda: piece(i, 0, high), up)
+
     def att_start(i):
         send(("up_l", i), lambda: piece(i, 0, low), up)
         send(("down_h", i), lambda: piece(i, 0, high), down)
@@ -528,10 +536,11 @@
     attend(0, 0)
     ring_step("o", 0, ((0, -1),) + going_south)
     attend(0, 1)
+    att_low(0)
     with jax.named_scope("attend0b"):
         attend(0, 2)
         attend(0, 3)
-    att_start(0)
+    att_high(0)
     with jax.named_scope("attend1a"):
         attend(1, 0)
         attend(1, 1)

time: 62.9 us -> 63 us (level)
  no operation moved by 1% of the time
where the time goes in v6:
time: 63 us; the launch traced here: 62.9 us
  Pallas kernels  62.1 us (99%)
  local copies, waits for them, and re-layouts  0.8 us (1%)
    pallas_call x1, Pallas kernels, body(): pl.pallas_call(functools.partial(tick_kernel, n_pipe, n_y), out_shape=plt...  62.1 us

profile of v6, /device:TPU:1, one launch (start us, length us, event | category | flops | bytes accessed | tf_op | source)
XLA Modules:
  0.0 62.9 jit_solution(16633593898501634457)
XLA Ops:
  0.0 62.1 %tick.1 = bf16[128,2048]{1,0:T(8,128)(2,1)S(1)} custom-call(s32[8,16]{1,0:T(8,128)} %bitcast.9, f32[1,2048]{1,0:T(1,128)} %gain_hbm.1, bf16[128,2048]{1,0:T(8,128)(2,1)} %bitcast.6, bf16[64,1536]{1,0:T(8,128)(2,1)} %bitcast.7, bf16[32,2048]{1,0:T(8,128)(2,1)} %bitcast.8), custom_call_target="tpu_custom_call" | custom-call | tf_op jit(solution)/shard_map/tick/pallas_call | solution.py:586
  62.1 0.8 %copy.7 = bf16[1,128,2048]{2,1,0:T(8,128)(2,1)} copy(bf16[1,128,2048]{2,1,0:T(8,128)(2,1)S(1)} %bitcast.5) | data formatting | bytes 1048576
